TPU v7x, 32 devices: a whole 2x2x4 slice. The times are simulated.
32 devices in a mesh: dp: 2 (over x), tp: 4 (over z), sp: 4 (over y, core).
Axes of the slice: x: 2, y: 2, z: 4, core: 2. Of those that a mesh axis runs over, the one named last changes fastest.
Arguments:
- hidden: bfloat16 [4, 128, 2048], P(None, 'dp'), parts along dimension 1
- start_pos: int32 [128], P('dp'), parts along dimension 0
- k_cache: bfloat16 [128, 1024, 8, 128], P('dp', 'sp', 'tp'), parts along dimension 0
- v_cache: bfloat16 [128, 1024, 8, 128], P('dp', 'sp', 'tp'), parts along dimension 0
- w_q: bfloat16 [2048, 2048], P(None, 'tp')
- w_k: bfloat16 [2048, 1024], P(None, 'tp')
- w_v: bfloat16 [2048, 1024], P(None, 'tp')
- w_o: bfloat16 [2048, 2048], P('tp')
- w_gate: bfloat16 [2048, 6144], P(None, 'tp')
- w_up: bfloat16 [2048, 6144], P(None, 'tp')
- w_down: bfloat16 [6144, 2048], P('tp')
- attn_norm: bfloat16 [2048], replicated
- mlp_norm: bfloat16 [2048], replicated
- q_gain: bfloat16 [128], replicated
- k_gain: bfloat16 [128], replicated
Outputs:
- output 1: bfloat16 [4, 128, 2048], P(None, 'dp'), parts along dimension 1
- output 2: bfloat16 [128, 1024, 8, 128], P('dp', 'sp', 'tp'), parts along dimension 0
- output 3: bfloat16 [128, 1024, 8, 128], P('dp', 'sp', 'tp'), parts along dimension 0
There are 2 independent parts. A program takes and returns all parts, laid end to end along the dimension named above; an argument that names none is the same for every part.
All inputs are finite; a program needn't handle non-finite values.
Results may differ from a plain program's by a relative error of at most 0.00853494.
Values sent between devices are 32-bit elements.
A program may use at most 1 GiB of HBM per device.

v0:
```python
import jax
import jax.numpy as jnp
from jax import lax
from jax.sharding import PartitionSpec as P

ROPE_BASE = 1000000.0
NORM_EPS = 1e-06
NEG_BIG = -1e30


def rms_scale(values, gain_vec):
    wide_vals = values.astype(jnp.float32)
    inv_rms = lax.rsqrt(jnp.mean(wide_vals * wide_vals, axis=-1, keepdims=True) + NORM_EPS)
    return wide_vals * inv_rms * gain_vec.astype(jnp.float32)


def apply_rope(vector, tok_pos):
    head_dim = vector.shape[-1]
    half_dim = head_dim // 2
    freqs = ROPE_BASE ** (-(jnp.arange(half_dim, dtype=jnp.float32) * (2.0 / head_dim)))
    angles = tok_pos.astype(jnp.float32)[:, None] * freqs[None, :]
    cos_tab = jnp.cos(angles)[:, None, :]
    sin_tab = jnp.sin(angles)[:, None, :]
    lower_half = vector[..., :half_dim]
    upper_half = vector[..., half_dim:]
    return jnp.concatenate([lower_half * cos_tab - upper_half * sin_tab, upper_half * cos_tab + lower_half * sin_tab], axis=-1)


def solution(mesh):
    cache_spec = P('dp', 'sp', 'tp', None)
    col_spec = P(None, 'tp')
    row_spec = P('tp', None)
    in_specs = (P(None, 'dp', None), P('dp'), cache_spec, cache_spec, col_spec, col_spec, col_spec, row_spec,
                col_spec, col_spec, row_spec, P(), P(), P(), P())
    out_specs = (P(None, 'dp', None), cache_spec, cache_spec)

    def shard_body(hidden, start_pos, k_cache, v_cache, w_q, w_k, w_v, w_o, w_gate, w_up, w_down, attn_norm, mlp_norm, q_gain, k_gain):
        n_steps, n_batch = hidden.shape[0], hidden.shape[1]
        seq_blk, kv_loc, head_dim = k_cache.shape[1], k_cache.shape[2], k_cache.shape[3]
        heads_loc = w_q.shape[1] // head_dim
        groups = heads_loc // kv_loc
        score_scale = head_dim ** -0.5
        blk_start = lax.axis_index('sp') * seq_blk
        blk_pos = blk_start + jnp.arange(seq_blk)
        old_mask = (blk_pos[None, :] < start_pos[:, None])[:, None, None, :]
        new_keys = []
        new_vals = []
        owned = []
        outputs = []
        for step_idx in range(n_steps):
            tok_pos = start_pos + step_idx
            x_tok = hidden[step_idx]
            normed = rms_scale(x_tok, attn_norm).astype(jnp.bfloat16)
            q_raw = jnp.dot(normed, w_q, preferred_element_type=jnp.float32).reshape(n_batch, heads_loc, head_dim)
            k_raw = jnp.dot(normed, w_k, preferred_element_type=jnp.float32).reshape(n_batch, kv_loc, head_dim)
            v_new = jnp.dot(normed, w_v, preferred_element_type=jnp.float32).astype(jnp.bfloat16).reshape(n_batch, kv_loc, head_dim)
            q_rot = apply_rope(rms_scale(q_raw, q_gain), tok_pos).astype(jnp.bfloat16).reshape(n_batch, kv_loc, groups, head_dim)
            k_new = apply_rope(rms_scale(k_raw, k_gain), tok_pos).astype(jnp.bfloat16)
            new_keys.append(k_new)
            new_vals.append(v_new)
            owned.append((tok_pos >= blk_start) & (tok_pos < blk_start + seq_blk))
            key_stack = jnp.stack(new_keys, axis=1)
            val_stack = jnp.stack(new_vals, axis=1)
            new_mask = jnp.stack(owned, axis=1)[:, None, None, :]
            old_scores = jnp.einsum('bkgh,bskh->bkgs', q_rot, k_cache, preferred_element_type=jnp.float32) * score_scale
            old_scores = jnp.where(old_mask, old_scores, NEG_BIG)
            new_scores = jnp.einsum('bkgh,bjkh->bkgj', q_rot, key_stack, preferred_element_type=jnp.float32) * score_scale
            new_scores = jnp.where(new_mask, new_scores, NEG_BIG)
            blk_max = jnp.maximum(old_scores.max(axis=-1), new_scores.max(axis=-1))
            old_probs = jnp.where(old_mask, jnp.exp(old_scores - blk_max[..., None]), 0.0)
            new_probs = jnp.where(new_mask, jnp.exp(new_scores - blk_max[..., None]), 0.0)
            blk_sum = old_probs.sum(axis=-1) + new_probs.sum(axis=-1)
            blk_out = (jnp.einsum('bkgs,bskh->bkgh', old_probs.astype(jnp.bfloat16), v_cache, preferred_element_type=jnp.float32)
                       + jnp.einsum('bkgj,bjkh->bkgh', new_probs.astype(jnp.bfloat16), val_stack, preferred_element_type=jnp.float32))
            packed = jnp.concatenate([blk_out, blk_max[..., None], blk_sum[..., None]], axis=-1)
            gathered = lax.all_gather(packed, 'sp')
            shard_max = gathered[..., head_dim]
            top_max = shard_max.max(axis=0)
            weights = jnp.exp(shard_max - top_max)
            total = (weights * gathered[..., head_dim + 1]).sum(axis=0)
            attn_vals = (weights[..., None] * gathered[..., :head_dim]).sum(axis=0) / total[..., None]
            attn_in = attn_vals.reshape(n_batch, heads_loc * head_dim).astype(jnp.bfloat16)
            attn_out = lax.psum(jnp.dot(attn_in, w_o, preferred_element_type=jnp.float32), 'tp')
            residual = (x_tok.astype(jnp.float32) + attn_out).astype(jnp.bfloat16)
            mlp_in = rms_scale(residual, mlp_norm).astype(jnp.bfloat16)
            gate_act = jnp.dot(mlp_in, w_gate, preferred_element_type=jnp.float32)
            up_proj = jnp.dot(mlp_in, w_up, preferred_element_type=jnp.float32)
            mlp_act = (jax.nn.silu(gate_act) * up_proj).astype(jnp.bfloat16)
            down_sum = lax.psum(jnp.dot(mlp_act, w_down, preferred_element_type=jnp.float32), 'tp')
            outputs.append((residual.astype(jnp.float32) + down_sum).astype(jnp.bfloat16))
        offsets = blk_pos[None, :] - start_pos[:, None]
        k_out = k_cache
        v_out = v_cache
        for step_idx in range(n_steps):
            hit = (offsets == step_idx)[:, :, None, None]
            k_out = jnp.where(hit, new_keys[step_idx][:, None], k_out)
            v_out = jnp.where(hit, new_vals[step_idx][:, None], v_out)
        return jnp.stack(outputs), k_out, v_out

    return jax.shard_map(shard_body, mesh=mesh, in_specs=in_specs, out_specs=out_specs, check_vma=False)
```

profile of v0, /device:TPU:1, one launch (start us, length us, event | category | flops | bytes accessed | tf_op | source)
XLA Modules:
  0.0 467.6 jit_solution(7475463987698842207)
XLA Ops:
  8.4 1.5 fusion.65
  10.6 1.6 convolution_convert_fusion.3
  12.9 2.3 convolution_convert_fusion.1
  15.2 2.3 convolution_convert_fusion
  17.5 2.3 copy.499
  19.7 1.8 multiply_reduce_fusion.8
  21.5 1.8 multiply_reduce_fusion.9
  23.3 1.6 convolution_convert_fusion.2
  24.8 1.8 multiply_reduce_fusion.10
  26.6 1.8 multiply_reduce_fusion.11
  28.4 4.1 copy.498
  32.5 3.1 multiply_reduce_fusion.4
  35.7 3.0 multiply_reduce_fusion.5
  38.7 3.0 multiply_reduce_fusion.6
  48.9 1.5 multiply_cosine_fusion.2
  52.0 1.9 multiply_multiply_fusion.2
  56.2 1.6 copy.426
  60.4 1.6 subtract_convert_fusion.5
  64.5 1.6 subtract_convert_fusion.4
  69.5 7.1 %fusion.250 = (f32[64,2,2]{2,1,0:T(2,128)}, f32[64,2,2,256]{3,2,1,0:T(2,128)}) fusion(bf16[64,256,2,128]{3,2,1,0:T(2,128)(2,1)} %param.17, bf16[64,2,2,64]{3,2,1,0:T(2,128)(2,1)} %copy-done.47, bf16[64,2,2,64]{3,2,1,0:T(2,128)(2,1)} %copy-done.46, pred[64,256]{1,0:T(8,128)(4,1)S(1)} %get-tuple-element.72), kind=kOutput, calls=%fused_computation.375 | convolution fusion | flops 17104640 | bytes 8733696 | tf_op jit(solution)/shard_map/bkgh,bskh->bkgs/dot_general | solution.py:65
  76.6 6.5 %fusion.245 = (f32[64,2,2]{2,1,0:T(2,128)S(1)}, f32[64,2,2,256]{3,2,1,0:T(2,128)}) fusion(bf16[64,256,2,128]{3,2,1,0:T(2,128)(2,1)} %param.17, bf16[64,2,2,64]{3,2,1,0:T(2,128)(2,1)S(1)} %copy.411, bf16[64,2,2,64]{3,2,1,0:T(2,128)(2,1)S(1)} %copy.410, pred[64,256]{1,0:T(8,128)(4,1)S(1)} %get-tuple-element.72), kind=kOutput, calls=%fused_computation.370 | convolution fusion | flops 17104640 | bytes 8733696 | tf_op jit(solution)/shard_map/bkgh,bskh->bkgs/dot_general | solution.py:65
  87.7 6.0 %fusion.246 = (f32[64,2,2]{2,1,0:T(2,128)S(1)}, f32[64,2,2,256]{3,2,1,0:T(2,128)S(1)}) fusion(bf16[64,256,2,128]{3,2,1,0:T(2,128)(2,1)} %param.17, bf16[64,2,2,64]{3,2,1,0:T(2,128)(2,1)} %copy.457, bf16[64,2,2,64]{3,2,1,0:T(2,128)(2,1)} %copy.456, pred[64,256]{1,0:T(8,128)(4,1)S(1)} %get-tuple-element.72), kind=kOutput, calls=%fused_computation.371 | convolution fusion | flops 17104640 | bytes 8733696 | tf_op jit(solution)/shard_map/bkgh,bskh->bkgs/dot_general | solution.py:65
  94.9 6.2 %fusion.248 = (f32[64,2,2]{2,1,0:T(2,128)S(1)}, f32[64,2,2,256]{3,2,1,0:T(2,128)S(1)}) fusion(bf16[64,256,2,128]{3,2,1,0:T(2,128)(2,1)} %param.17, bf16[64,2,2,64]{3,2,1,0:T(2,128)(2,1)S(1)} %copy-done.45, bf16[64,2,2,64]{3,2,1,0:T(2,128)(2,1)S(1)} %copy-done.44, pred[64,256]{1,0:T(8,128)(4,1)S(1)} %get-tuple-element.72), kind=kOutput, calls=%fused_computation.373 | convolution fusion | flops 17104640 | bytes 8733696 | tf_op jit(solution)/shard_map/bkgh,bskh->bkgs/dot_general | solution.py:65
  102.2 1.9 fusion.4
  104.1 1.9 fusion.2
  106.1 1.9 fusion
  108.0 2.3 fusion.206
  115.0 1.5 add_bitcast_fusion.2
  116.5 2.3 copy.437
  118.9 1.5 add_bitcast_fusion.3
  120.4 2.3 copy.418
  122.7 1.5 copy.436
  126.7 11.4 %all-gather.1 = f32[256,2,2,130]{3,2,1,0:T(2,128)S(1)} all-gather(f32[64,2,2,130]{3,2,1,0:T(2,128)S(1)} %pad_maximum_fusion.2), channel_id=3, replica_groups=mesh['dp'=2,'tp'=4,'sp'=4] {'sp'}, dimensions={0}, use_global_device_ids=true | all-gather | bytes 665600 | tf_op jit(solution)/shard_map/all_gather | solution.py:76
  139.1 4.7 %fusion.34 = f32[64,2,2,128]{3,2,1,0:T(2,128)S(1)} fusion(bf16[64,256,2,128]{3,2,1,0:T(2,128)(2,1)} %param.18, f32[64,2,128]{2,1,0:T(2,128)} %convert.87, f32[64,2,2]{2,1,0:T(2,128)} %get-tuple-element.27, f32[64,2,2,256]{3,2,1,0:T(2,128)} %get-tuple-element.120, pred[64,256]{1,0:T(8,128)(4,1)S(1)} %get-tuple-element.72, f32[64,2,2]{2,1,0:T(2,128)S(1)} %get-tuple-element.29), kind=kOutput, calls=%fused_computation.43 | convolution fusion | flops 17039360 | bytes 8865792 | tf_op jit(solution)/shard_map/bkgs,bskh->bkgh/dot_general | solution.py:73
  144.1 10.5 %all-gather = f32[256,2,2,130]{3,2,1,0:T(2,128)S(1)} all-gather(f32[64,2,2,130]{3,2,1,0:T(2,128)S(1)} %pad_maximum_fusion.1), channel_id=2, replica_groups=mesh['dp'=2,'tp'=4,'sp'=4] {'sp'}, dimensions={0}, use_global_device_ids=true | all-gather | bytes 665600 | tf_op jit(solution)/shard_map/all_gather | solution.py:76
  155.6 3.7 fusion.241
  160.6 1.9 fusion.219
  164.0 1.9 fusion.220
  165.9 1.5 copy.469
  168.3 1.5 copy.470
  172.3 1.6 convolution_add_fusion.1
  175.1 10.1 %all-gather.2 = f32[256,2,2,130]{3,2,1,0:T(2,128)S(1)} all-gather(f32[64,2,2,130]{3,2,1,0:T(2,128)S(1)} %pad_maximum_fusion.3), channel_id=4, replica_groups=mesh['dp'=2,'tp'=4,'sp'=4] {'sp'}, dimensions={0}, use_global_device_ids=true | all-gather | bytes 665600 | tf_op jit(solution)/shard_map/all_gather | solution.py:76
  187.0 10.3 %all-gather.3 = f32[256,2,2,130]{3,2,1,0:T(2,128)S(1)} all-gather(f32[64,2,2,130]{3,2,1,0:T(2,128)S(1)} %pad_maximum_fusion.4), channel_id=5, replica_groups=mesh['dp'=2,'tp'=4,'sp'=4] {'sp'}, dimensions={0}, use_global_device_ids=true | all-gather | bytes 665600 | tf_op jit(solution)/shard_map/all_gather | solution.py:76
  198.3 3.7 fusion.243
  202.1 2.2 copy.506
  204.2 2.2 copy.509
  211.7 2.2 copy.503
  213.9 2.0 multiply_reduce_fusion.2
  217.2 2.0 multiply_reduce_fusion.3
  225.9 2.0 multiply_reduce_fusion.1
  229.2 2.2 copy.512
  231.4 2.0 multiply_reduce_fusion
  239.6 80.4 %all-reduce.7.cloned.1.call-done = (f32[64,2048]{1,0:T(8,128)}, f32[64,2048]{1,0:T(8,128)}, f32[64,2048]{1,0:T(8,128)}, f32[64,2048]{1,0:T(8,128)}) async-done(((f32[64,2048]{1,0:T(8,128)}, f32[64,2048]{1,0:T(8,128)}, f32[64,2048]{1,0:T(8,128)}, f32[64,2048]{1,0:T(8,128)}), (f32[64,2048]{1,0:T(8,128)}, f32[64,2048]{1,0:T(8,128)}, f32[64,2048]{1,0:T(8,128)}, ...) | async-done | bytes 2097168 | tf_op jit(solution)/shard_map/psum | solution.py:83
  320.1 2.0 fusion.89
  322.2 4.3 fusion.169
  326.5 4.0 fusion.173
  330.5 7.8 %fusion.49 = f32[64,2048]{1,0:T(8,128)} fusion(bf16[1536,2048]{1,0:T(8,128)(2,1)} %param.25, bf16[2048,1536]{1,0:T(8,128)(2,1)} %param.24, f32[64,1536]{1,0:T(8,128)S(1)} %fusion.169, bf16[64,2048]{1,0:T(8,128)(2,1)S(1)} %get-tuple-element.37, f32[64]{0:T(128)S(1)} %add_rsqrt_fusion.8, f32[2048]{0:T(1024)S(1)} %convert_element_type.307), kind=kOutput, calls=%fused_computation.57 | convolution fusion | flops 806420480 | bytes 13771008 | tf_op jit(solution)/shard_map/dot_general | solution.py:89
  338.3 7.8 %fusion.50 = f32[64,2048]{1,0:T(8,128)} fusion(bf16[1536,2048]{1,0:T(8,128)(2,1)} %param.25, bf16[2048,1536]{1,0:T(8,128)(2,1)} %param.24, f32[64,1536]{1,0:T(8,128)S(1)} %fusion.173, bf16[64,2048]{1,0:T(8,128)(2,1)S(1)} %get-tuple-element.35, f32[64]{0:T(128)S(1)} %add_rsqrt_fusion.10, f32[2048]{0:T(1024)S(1)} %convert_element_type.307), kind=kOutput, calls=%fused_computation.58 | convolution fusion | flops 806420480 | bytes 13771008 | tf_op jit(solution)/shard_map/dot_general | solution.py:89
  346.0 4.0 fusion.177
  350.1 7.8 %fusion.51 = f32[64,2048]{1,0:T(8,128)} fusion(bf16[1536,2048]{1,0:T(8,128)(2,1)} %param.25, bf16[2048,1536]{1,0:T(8,128)(2,1)} %param.24, f32[64,1536]{1,0:T(8,128)S(1)} %fusion.177, bf16[64,2048]{1,0:T(8,128)(2,1)S(1)} %get-tuple-element.33, f32[64]{0:T(128)S(1)} %add_rsqrt_fusion.12, f32[2048]{0:T(1024)S(1)} %convert_element_type.307), kind=kOutput, calls=%fused_computation.59 | convolution fusion | flops 806420480 | bytes 13771008 | tf_op jit(solution)/shard_map/dot_general | solution.py:89
  357.9 4.0 fusion.181
  362.0 7.8 %fusion.52 = f32[64,2048]{1,0:T(8,128)} fusion(bf16[1536,2048]{1,0:T(8,128)(2,1)} %param.25, bf16[2048,1536]{1,0:T(8,128)(2,1)} %param.24, f32[64,1536]{1,0:T(8,128)S(1)} %fusion.181, bf16[64,2048]{1,0:T(8,128)(2,1)S(1)} %get-tuple-element.20, f32[2048]{0:T(1024)S(1)} %convert_element_type.307, f32[64]{0:T(128)S(1)} %add_rsqrt_fusion.14), kind=kOutput, calls=%fused_computation.60 | convolution fusion | flops 806420480 | bytes 13771008 | tf_op jit(solution)/shard_map/dot_general | solution.py:89
  369.9 77.8 %broadcast_select_fusion.6 = (bf16[64,256,2,128]{3,2,1,0:T(2,128)(2,1)}, bf16[64,256,2,128]{3,2,1,0:T(2,128)(2,1)}) fusion(pred[64,256]{1,0:T(8,128)(4,1)S(1)} %copy-done.37, pred[64,256]{1,0:T(8,128)(4,1)S(1)} %copy-done.39, pred[64,256]{1,0:T(8,128)(4,1)S(1)} %copy-done.38, bf16[64,256,2,128]{3,2,1,0:T(2,128)(2,1)} %param.18, ...), kind=kLoop, calls=%fused_computation.6 | loop fusion | flops 33554432 | bytes 33882112 | tf_op jit(solution)/shard_map/jit(_where)/select_n | solution.py:97
  447.7 7.3 %all-reduce.5.cloned.1.call-done = (f32[64,2048]{1,0:T(8,128)}, f32[64,2048]{1,0:T(8,128)}, f32[64,2048]{1,0:T(8,128)}, f32[64,2048]{1,0:T(8,128)}) async-done(((f32[64,2048]{1,0:T(8,128)}, f32[64,2048]{1,0:T(8,128)}, f32[64,2048]{1,0:T(8,128)}, f32[64,2048]{1,0:T(8,128)}), (f32[64,2048]{1,0:T(8,128)}, f32[64,2048]{1,0:T(8,128)}, f32[64,2048]{1,0:T(8,128)}, ...) | async-done | bytes 2097168 | tf_op jit(solution)/shard_map/psum | solution.py:89
  (269 shorter events, 74.4 us)
Async XLA Ops:
  7.2 208.8 %copy-start = (bf16[512,2048]{1,0:T(8,128)(2,1)S(1)}, bf16[512,2048]{1,0:T(8,128)(2,1)}, u32[]{:S(2)}) copy-start(bf16[512,2048]{1,0:T(8,128)(2,1)} %param.22) | copy-start | bytes 6291460
  7.2 12.5 %copy-start.3 = (bf16[4,64,2048]{2,1,0:T(8,128)(2,1)S(1)}, bf16[4,64,2048]{2,1,0:T(8,128)(2,1)}, u32[]{:S(2)}) copy-start(bf16[4,64,2048]{2,1,0:T(8,128)(2,1)} %param.15) | copy-start | bytes 3145732
  7.2 312.9 %all-reduce.7.cloned.1.call-start = ((), (), s32[]{:S(2)}) async-start(), calls=%async_computation.1 | async-start | bytes 4194304 | tf_op jit(solution)/shard_map/psum | solution.py:83
  12.3 34.5 %copy-start.26 = (bf16[64,2,128]{2,1,0:T(2,128)(2,1)}, bf16[64,2,128]{2,1,0:T(2,128)(2,1)S(1)}, u32[]{:S(2)}) copy-start(bf16[64,2,128]{2,1,0:T(2,128)(2,1)S(1)} %reshape.881) | copy-start | bytes 98308
  24.8 21.3 %copy-start.21 = (bf16[64,256]{1,0:T(8,128)(2,1)}, bf16[64,256]{1,0:T(8,128)(2,1)S(1)}, u32[]{:S(2)}) copy-start(bf16[64,256]{1,0:T(8,128)(2,1)S(1)} %convolution_convert_fusion.2) | copy-start | bytes 98308
  28.4 14.8 %copy-start.62 = (bf16[128]{0:T(256)(128)(2,1)S(1)}, bf16[128]{0:T(256)(128)(2,1)}, u32[]{:S(2)}) copy-start(bf16[128]{0:T(256)(128)(2,1)} %param.28) | copy-start | bytes 772
  28.4 15.2 %copy-start.63 = (bf16[128]{0:T(256)(128)(2,1)S(1)}, bf16[128]{0:T(256)(128)(2,1)}, u32[]{:S(2)}) copy-start(bf16[128]{0:T(256)(128)(2,1)} %param.29) | copy-start | bytes 772
  28.4 15.8 %copy-start.59 = (s32[64]{0:T(128)S(1)}, s32[64]{0:T(128)}, u32[]{:S(2)}) copy-start(s32[64]{0:T(128)} %param.16) | copy-start | bytes 772
  32.5 9.2 %copy-start.2 = (bf16[512,2048]{1,0:T(8,128)(2,1)S(1)}, bf16[512,2048]{1,0:T(8,128)(2,1)}, u32[]{:S(2)}) copy-start(bf16[512,2048]{1,0:T(8,128)(2,1)} %copy.498) | copy-start | bytes 6291460
  44.2 6.3 %copy-start.56 = (pred[64]{0:T(512)(128)(4,1)}, pred[64]{0:T(512)(128)(4,1)S(1)}, u32[]{:S(2)}) copy-start(pred[64]{0:T(512)(128)(4,1)S(1)} %get-tuple-element.88) | copy-start | bytes 196
  76.6 6.5 %copy-start.51 = (bf16[64,2,128,1]{2,0,1,3:T(8,128)(2,1)S(1)}, bf16[64,2,128,1]{2,0,1,3:T(8,128)(2,1)}, u32[]{:S(2)}) copy-start(bf16[64,2,128,1]{2,0,1,3:T(8,128)(2,1)} %fusion.288) | copy-start | bytes 98308
  76.6 6.9 %copy-start.57 = (pred[64]{0:T(512)(128)(4,1)S(1)}, pred[64]{0:T(512)(128)(4,1)}, u32[]{:S(2)}) copy-start(pred[64]{0:T(512)(128)(4,1)} %copy-done.56) | copy-start | bytes 196
  76.6 10.8 %copy-start.14 = (bf16[64,2,64]{2,0,1:T(8,128)(2,1)S(1)}, bf16[64,2,64]{2,0,1:T(8,128)(2,1)}, u32[]{:S(2)}) copy-start(bf16[64,2,64]{2,0,1:T(8,128)(2,1)} %get-tuple-element.60) | copy-start | bytes 49156
  76.6 10.8 %copy-start.16 = (bf16[64,2,64]{2,0,1:T(8,128)(2,1)S(1)}, bf16[64,2,64]{2,0,1:T(8,128)(2,1)}, u32[]{:S(2)}) copy-start(bf16[64,2,64]{2,0,1:T(8,128)(2,1)} %get-tuple-element.61) | copy-start | bytes 49156
  76.6 10.9 %copy-start.22 = (bf16[64,2,64]{2,0,1:T(8,128)(2,1)S(1)}, bf16[64,2,64]{2,0,1:T(8,128)(2,1)}, u32[]{:S(2)}) copy-start(bf16[64,2,64]{2,0,1:T(8,128)(2,1)} %get-tuple-element.62) | copy-start | bytes 49156
  76.6 10.9 %copy-start.23 = (bf16[64,2,64]{2,0,1:T(8,128)(2,1)S(1)}, bf16[64,2,64]{2,0,1:T(8,128)(2,1)}, u32[]{:S(2)}) copy-start(bf16[64,2,64]{2,0,1:T(8,128)(2,1)} %get-tuple-element.63) | copy-start | bytes 49156
  87.4 6.3 %copy-start.48 = (bf16[64,2,2,64]{3,2,1,0:T(2,128)(2,1)S(1)}, bf16[64,2,2,64]{3,2,1,0:T(2,128)(2,1)}, u32[]{:S(2)}) copy-start(bf16[64,2,2,64]{3,2,1,0:T(2,128)(2,1)} %copy.456) | copy-start | bytes 98308
  87.4 6.4 %copy-start.49 = (bf16[64,2,2,64]{3,2,1,0:T(2,128)(2,1)S(1)}, bf16[64,2,2,64]{3,2,1,0:T(2,128)(2,1)}, u32[]{:S(2)}) copy-start(bf16[64,2,2,64]{3,2,1,0:T(2,128)(2,1)} %copy.457) | copy-start | bytes 98308
  87.4 6.4 %copy-start.52 = (pred[64,4]{1,0:T(8,128)(4,1)S(1)}, pred[64,4]{1,0:T(8,128)(4,1)}, u32[]{:S(2)}) copy-start(pred[64,4]{1,0:T(8,128)(4,1)} %copy.459) | copy-start | bytes 772
  87.4 7.4 %copy-start.44 = (bf16[64,2,2,64]{3,2,1,0:T(2,128)(2,1)S(1)}, bf16[64,2,2,64]{3,2,1,0:T(2,128)(2,1)}, u32[]{:S(2)}) copy-start(bf16[64,2,2,64]{3,2,1,0:T(2,128)(2,1)} %copy.440) | copy-start | bytes 98308
  87.4 7.4 %copy-start.45 = (bf16[64,2,2,64]{3,2,1,0:T(2,128)(2,1)S(1)}, bf16[64,2,2,64]{3,2,1,0:T(2,128)(2,1)}, u32[]{:S(2)}) copy-start(bf16[64,2,2,64]{3,2,1,0:T(2,128)(2,1)} %copy.441) | copy-start | bytes 98308
  87.7 14.5 %slice-start = ((s8[8388608]{0:T(1024)(128)(4,1)}), s8[4194304]{0:T(1024)(128)(4,1)S(1)}, s32[]{:S(2)}) async-start(s8[8388608]{0:T(1024)(128)(4,1)} %bitcast.256), calls=%async_computation.2 | async-start | bytes 8388608
  93.8 7.3 %copy-start.54 = (pred[64,3]{1,0:T(8,128)(4,1)S(1)}, pred[64,3]{1,0:T(8,128)(4,1)}, u32[]{:S(2)}) copy-start(pred[64,3]{1,0:T(8,128)(4,1)} %copy.443) | copy-start | bytes 580
  93.8 8.4 %copy-start.31 = (f32[64,2,2,256]{3,2,1,0:T(2,128)S(1)}, f32[64,2,2,256]{3,2,1,0:T(2,128)}, u32[]{:S(2)}) copy-start(f32[64,2,2,256]{3,2,1,0:T(2,128)} %get-tuple-element.130) | copy-start | bytes 786436
  94.9 7.3 %slice-start.1 = ((s8[8388608]{0:T(1024)(128)(4,1)}), s8[4194304]{0:T(1024)(128)(4,1)S(1)}, s32[]{:S(2)}) async-start(s8[8388608]{0:T(1024)(128)(4,1)} %bitcast.256), calls=%async_computation.3 | async-start | bytes 8388608
  106.0 4.3 copy-start.50
  106.0 4.3 copy-start.58
  106.0 4.3 copy-start.61
  139.1 4.7 %copy-start.10 = (f32[64,2,2,1]{3,2,1,0:T(2,128)S(1)}, f32[64,2,2,1]{3,2,1,0:T(2,128)}, u32[]{:S(2)}) copy-start(f32[64,2,2,1]{3,2,1,0:T(2,128)} %copy.417) | copy-start | bytes 3076
  139.1 4.7 %copy-start.13 = (f32[64,2,2,1]{3,2,1,0:T(2,128)S(1)}, f32[64,2,2,1]{3,2,1,0:T(2,128)}, u32[]{:S(2)}) copy-start(f32[64,2,2,1]{3,2,1,0:T(2,128)} %copy.418) | copy-start | bytes 3076
  143.8 15.5 %copy-start.20 = (bf16[64,256]{1,0:T(8,128)(2,1)S(1)}, bf16[64,256]{1,0:T(8,128)(2,1)}, u32[]{:S(2)}) copy-start(bf16[64,256]{1,0:T(8,128)(2,1)} %convolution_convert_fusion) | copy-start | bytes 98308
  143.8 16.1 %copy-start.18 = (bf16[64,256]{1,0:T(8,128)(2,1)S(1)}, bf16[64,256]{1,0:T(8,128)(2,1)}, u32[]{:S(2)}) copy-start(bf16[64,256]{1,0:T(8,128)(2,1)} %convolution_convert_fusion.1) | copy-start | bytes 98308
  143.9 16.7 %copy-start.55 = (pred[64,3]{1,0:T(8,128)(4,1)S(1)}, pred[64,3]{1,0:T(8,128)(4,1)}, u32[]{:S(2)}) copy-start(pred[64,3]{1,0:T(8,128)(4,1)} %copy.443) | copy-start | bytes 580
  143.9 20.1 %copy-start.53 = (pred[64,4]{1,0:T(8,128)(4,1)S(1)}, pred[64,4]{1,0:T(8,128)(4,1)}, u32[]{:S(2)}) copy-start(pred[64,4]{1,0:T(8,128)(4,1)} %copy.459) | copy-start | bytes 772
  172.2 14.0 %copy-start.32 = (f32[64,2,2,4]{3,2,1,0:T(2,128)S(1)}, f32[64,2,2,4]{3,2,1,0:T(2,128)}, u32[]{:S(2)}) copy-start(f32[64,2,2,4]{3,2,1,0:T(2,128)} %get-tuple-element.124) | copy-start | bytes 12292
  172.2 14.0 %copy-start.40 = (bf16[64,1,2,128]{3,1,2,0:T(2,128)(2,1)S(1)}, bf16[64,1,2,128]{3,1,2,0:T(2,128)(2,1)}, u32[]{:S(2)}) copy-start(bf16[64,1,2,128]{3,1,2,0:T(2,128)(2,1)} %stack_reshape.23) | copy-start | bytes 98308
  172.3 14.0 %copy-start.41 = (bf16[64,1,2,128]{3,1,2,0:T(2,128)(2,1)S(1)}, bf16[64,1,2,128]{3,1,2,0:T(2,128)(2,1)}, u32[]{:S(2)}) copy-start(bf16[64,1,2,128]{3,1,2,0:T(2,128)(2,1)} %stack_reshape.24) | copy-start | bytes 98308
  172.3 14.0 %copy-start.42 = (bf16[64,1,2,128]{3,1,2,0:T(2,128)(2,1)S(1)}, bf16[64,1,2,128]{3,1,2,0:T(2,128)(2,1)}, u32[]{:S(2)}) copy-start(bf16[64,1,2,128]{3,1,2,0:T(2,128)(2,1)} %stack_reshape.22) | copy-start | bytes 98308
  172.3 14.0 %copy-start.43 = (bf16[64,1,2,128]{3,1,2,0:T(2,128)(2,1)S(1)}, bf16[64,1,2,128]{3,1,2,0:T(2,128)(2,1)}, u32[]{:S(2)}) copy-start(bf16[64,1,2,128]{3,1,2,0:T(2,128)(2,1)} %stack_reshape.25) | copy-start | bytes 98308
  172.3 14.0 %copy-start.64 = (f32[64,2,2,128]{3,2,1,0:T(2,128)S(1)}, f32[64,2,2,128]{3,2,1,0:T(2,128)}, u32[]{:S(2)}) copy-start(f32[64,2,2,128]{3,2,1,0:T(2,128)} %fusion) | copy-start | bytes 393220
  172.3 14.5 %copy-start.11 = (f32[64,2,2,1]{3,2,1,0:T(2,128)S(1)}, f32[64,2,2,1]{3,2,1,0:T(2,128)}, u32[]{:S(2)}) copy-start(f32[64,2,2,1]{3,2,1,0:T(2,128)} %copy.469) | copy-start | bytes 3076
  172.3 14.5 %copy-start.12 = (f32[64,2,2,1]{3,2,1,0:T(2,128)S(1)}, f32[64,2,2,1]{3,2,1,0:T(2,128)}, u32[]{:S(2)}) copy-start(f32[64,2,2,1]{3,2,1,0:T(2,128)} %copy.470) | copy-start | bytes 3076
  186.8 20.8 %copy-start.28 = (f32[64,2,2]{2,1,0:T(2,128)S(1)}, f32[64,2,2]{2,1,0:T(2,128)}, u32[]{:S(2)}) copy-start(f32[64,2,2]{2,1,0:T(2,128)} %get-tuple-element.39) | copy-start | bytes 3076
  207.8 13.9 %copy-start.29 = (f32[64,2,2]{2,1,0:T(2,128)S(1)}, f32[64,2,2]{2,1,0:T(2,128)}, u32[]{:S(2)}) copy-start(f32[64,2,2]{2,1,0:T(2,128)} %get-tuple-element.45) | copy-start | bytes 3076
  225.8 10.5 %copy-start.19 = (bf16[64,256]{1,0:T(8,128)(2,1)S(1)}, bf16[64,256]{1,0:T(8,128)(2,1)}, u32[]{:S(2)}) copy-start(bf16[64,256]{1,0:T(8,128)(2,1)} %convolution_convert_fusion.1) | copy-start | bytes 98308
  225.9 12.5 %copy-start.60 = (bf16[2048]{0:T(1024)(128)(2,1)S(1)}, bf16[2048]{0:T(1024)(128)(2,1)}, u32[]{:S(2)}) copy-start(bf16[2048]{0:T(1024)(128)(2,1)} %param.27) | copy-start | bytes 12292
  225.9 12.6 %copy-start.15 = (bf16[64,2,64]{2,0,1:T(8,128)(2,1)S(1)}, bf16[64,2,64]{2,0,1:T(8,128)(2,1)}, u32[]{:S(2)}) copy-start(bf16[64,2,64]{2,0,1:T(8,128)(2,1)} %get-tuple-element.60) | copy-start | bytes 49156
  225.9 12.6 %copy-start.17 = (bf16[64,2,64]{2,0,1:T(8,128)(2,1)S(1)}, bf16[64,2,64]{2,0,1:T(8,128)(2,1)}, u32[]{:S(2)}) copy-start(bf16[64,2,64]{2,0,1:T(8,128)(2,1)} %get-tuple-element.61) | copy-start | bytes 49156
  234.7 220.4 %all-reduce.5.cloned.1.call-start = ((), (), s32[]{:S(2)}) async-start(), calls=%async_computation | async-start | bytes 4194304 | tf_op jit(solution)/shard_map/psum | solution.py:89
  322.1 8.4 %copy-start.4 = (bf16[64,2048]{1,0:T(8,128)(2,1)}, bf16[64,2048]{1,0:T(8,128)(2,1)S(1)}, u32[]{:S(2)}) copy-start(bf16[64,2048]{1,0:T(8,128)(2,1)S(1)} %get-tuple-element.37) | copy-start | bytes 786436
  322.1 28.0 %copy-start.6 = (bf16[64,2048]{1,0:T(8,128)(2,1)}, bf16[64,2048]{1,0:T(8,128)(2,1)S(1)}, u32[]{:S(2)}) copy-start(bf16[64,2048]{1,0:T(8,128)(2,1)S(1)} %get-tuple-element.33) | copy-start | bytes 786436
  322.1 39.8 %copy-start.8 = (bf16[64,2048]{1,0:T(8,128)(2,1)}, bf16[64,2048]{1,0:T(8,128)(2,1)S(1)}, u32[]{:S(2)}) copy-start(bf16[64,2048]{1,0:T(8,128)(2,1)S(1)} %get-tuple-element.20) | copy-start | bytes 786436
  361.9 7.9 %copy-start.27 = (bf16[64,2,128]{2,1,0:T(2,128)(2,1)S(1)}, bf16[64,2,128]{2,1,0:T(2,128)(2,1)}, u32[]{:S(2)}) copy-start(bf16[64,2,128]{2,1,0:T(2,128)(2,1)} %copy-done.26) | copy-start | bytes 98308
  361.9 7.9 %copy-start.33 = (bf16[64,2,128]{2,1,0:T(2,128)(2,1)S(1)}, bf16[64,2,128]{2,1,0:T(2,128)(2,1)}, u32[]{:S(2)}) copy-start(bf16[64,2,128]{2,1,0:T(2,128)(2,1)} %broadcast_in_dim.329) | copy-start | bytes 98308
  361.9 7.9 %copy-start.34 = (bf16[64,2,128]{2,1,0:T(2,128)(2,1)S(1)}, bf16[64,2,128]{2,1,0:T(2,128)(2,1)}, u32[]{:S(2)}) copy-start(bf16[64,2,128]{2,1,0:T(2,128)(2,1)} %broadcast_in_dim.331) | copy-start | bytes 98308
  362.0 7.9 %copy-start.35 = (bf16[64,2,128]{2,1,0:T(2,128)(2,1)S(1)}, bf16[64,2,128]{2,1,0:T(2,128)(2,1)}, u32[]{:S(2)}) copy-start(bf16[64,2,128]{2,1,0:T(2,128)(2,1)} %broadcast_in_dim.333) | copy-start | bytes 98308
  362.0 7.9 %copy-start.36 = (pred[64,256]{1,0:T(8,128)(4,1)S(1)}, pred[64,256]{1,0:T(8,128)(4,1)}, u32[]{:S(2)}) copy-start(pred[64,256]{1,0:T(8,128)(4,1)} %get-tuple-element.68) | copy-start | bytes 49156
  362.0 7.9 %copy-start.37 = (pred[64,256]{1,0:T(8,128)(4,1)S(1)}, pred[64,256]{1,0:T(8,128)(4,1)}, u32[]{:S(2)}) copy-start(pred[64,256]{1,0:T(8,128)(4,1)} %get-tuple-element.69) | copy-start | bytes 49156
  362.0 7.9 %copy-start.38 = (pred[64,256]{1,0:T(8,128)(4,1)S(1)}, pred[64,256]{1,0:T(8,128)(4,1)}, u32[]{:S(2)}) copy-start(pred[64,256]{1,0:T(8,128)(4,1)} %get-tuple-element.70) | copy-start | bytes 49156
  362.0 7.9 %copy-start.39 = (pred[64,256]{1,0:T(8,128)(4,1)S(1)}, pred[64,256]{1,0:T(8,128)(4,1)}, u32[]{:S(2)}) copy-start(pred[64,256]{1,0:T(8,128)(4,1)} %get-tuple-element.71) | copy-start | bytes 49156
  369.9 85.1 %copy-start.9 = (bf16[64,2048]{1,0:T(8,128)(2,1)S(1)}, bf16[64,2048]{1,0:T(8,128)(2,1)}, u32[]{:S(2)}) copy-start(bf16[64,2048]{1,0:T(8,128)(2,1)} %copy-done.8) | copy-start | bytes 786436
  369.9 86.2 %copy-start.7 = (bf16[64,2048]{1,0:T(8,128)(2,1)S(1)}, bf16[64,2048]{1,0:T(8,128)(2,1)}, u32[]{:S(2)}) copy-start(bf16[64,2048]{1,0:T(8,128)(2,1)} %copy-done.6) | copy-start | bytes 786436
  369.9 87.3 %copy-start.5 = (bf16[64,2048]{1,0:T(8,128)(2,1)S(1)}, bf16[64,2048]{1,0:T(8,128)(2,1)}, u32[]{:S(2)}) copy-start(bf16[64,2048]{1,0:T(8,128)(2,1)} %copy-done.4) | copy-start | bytes 786436
  369.9 90.6 %copy-start.1 = (bf16[512,2048]{1,0:T(8,128)(2,1)S(1)}, bf16[512,2048]{1,0:T(8,128)(2,1)}, u32[]{:S(2)}) copy-start(bf16[512,2048]{1,0:T(8,128)(2,1)} %param.22) | copy-start | bytes 6291460
  (5 other events, 11.6 us)
Sparse Core Ops, SparseCore 0:
  234.8 85.2 all-reduce.6
  369.9 85.0 all-reduce.4
where the time goes:
time: 475 us; the launch traced here: 468 us
  other arithmetic  140 us (29%)
  matrix products  121 us (25%)
  waiting for transfers between devices  87.8 us (18%)
  local copies, waits for them, and re-layouts  60.3 us (13%)
  blocking collectives  42.4 us (9%)
  between operations  15.5 us (3%)
    psum x1, waiting for transfers between devices, shard_body(): lax.psum(jnp.dot(attn_in, w_o, preferred_element_type=jnp.float32), 'tp')  80.4 us
    select_n x1, other arithmetic, shard_body(): v_out = jnp.where(hit, new_vals[step_idx][:, None], v_out)  77.8 us
    all_gather x4, blocking collectives, shard_body(): gathered = lax.all_gather(packed, 'sp')  42.4 us
    dot_general x4, matrix products, shard_body(): jnp.dot(mlp_act, w_down, preferred_element_type=jnp.float32)  31.1 us
    dot_general x4, matrix products, shard_body(): jnp.einsum('bkgh,bskh->bkgs', q_rot, k_cache, preferred_element_type=jnp....  25.8 us
    unnamed x152, local copies, waits for them, and re-layouts  22.2 us
    dot_general x4, matrix products, shard_body(): gate_act = jnp.dot(mlp_in, w_gate, preferred_element_type=jnp.float32)  16.4 us
    dot_general x4, matrix products, shard_body(): jnp.dot(normed, w_q, preferred_element_type=jnp.float32)  10.6 us
  transfers between devices with their start and end apart: 2, of which 2 were waited for; matrix products, arithmetic and copies ran while one was open for 18% of the time, Pallas kernels for 0%

commit v1 on v0

v1 whole, which is shorter than its diff:
```python
import jax
import jax.numpy as jnp
from jax import lax
from jax.sharding import PartitionSpec as P

ROPE_BASE = 1000000.0
NORM_EPS = 1e-06
NEG_BIG = -1e30


def rms_scale(values, gain_vec):
    wide_vals = values.astype(jnp.float32)
    inv_rms = lax.rsqrt(jnp.mean(wide_vals * wide_vals, axis=-1, keepdims=True) + NORM_EPS)
    return wide_vals * inv_rms * gain_vec.astype(jnp.float32)


def apply_rope(vector, tok_pos):
    head_dim = vector.shape[-1]
    half_dim = head_dim // 2
    freqs = ROPE_BASE ** (-(jnp.arange(half_dim, dtype=jnp.float32) * (2.0 / head_dim)))
    angles = tok_pos.astype(jnp.float32)[:, None] * freqs[None, :]
    cos_tab = jnp.cos(angles)[:, None, :]
    sin_tab = jnp.sin(angles)[:, None, :]
    lower_half = vector[..., :half_dim]
    upper_half = vector[..., half_dim:]
    return jnp.concatenate([lower_half * cos_tab - upper_half * sin_tab, upper_half * cos_tab + lower_half * sin_tab], axis=-1)


def solution(mesh):
    cache_spec = P('dp', 'sp', 'tp', None)
    col_spec = P(None, 'tp')
    row_spec = P('tp', None)
    in_specs = (P(None, 'dp', None), P('dp'), cache_spec, cache_spec, col_spec, col_spec, col_spec, row_spec,
                col_spec, col_spec, row_spec, P(), P(), P(), P())
    out_specs = (P(None, 'dp', None), cache_spec, cache_spec)

    def shard_body(hidden, start_pos, k_cache, v_cache, w_q, w_k, w_v, w_o, w_gate, w_up, w_down, attn_norm, mlp_norm, q_gain, k_gain):
        n_steps, n_batch = hidden.shape[0], hidden.shape[1]
        seq_blk, kv_loc, head_dim = k_cache.shape[1], k_cache.shape[2], k_cache.shape[3]
        heads_loc = w_q.shape[1] // head_dim
        groups = heads_loc // kv_loc
        n_tok = n_steps * n_batch
        score_scale = head_dim ** -0.5
        blk_start = lax.axis_index('sp') * seq_blk
        blk_pos = blk_start + jnp.arange(seq_blk)
        tok_pos = (start_pos[None, :] + jnp.arange(n_steps, dtype=jnp.int32)[:, None]).reshape(n_tok)
        x_tok = hidden.reshape(n_tok, hidden.shape[2])
        normed = rms_scale(x_tok, attn_norm).astype(jnp.bfloat16)
        q_raw = jnp.dot(normed, w_q, preferred_element_type=jnp.float32).reshape(n_tok, heads_loc, head_dim)
        k_raw = jnp.dot(normed, w_k, preferred_element_type=jnp.float32).reshape(n_tok, kv_loc, head_dim)
        v_new = jnp.dot(normed, w_v, preferred_element_type=jnp.float32).astype(jnp.bfloat16).reshape(n_steps, n_batch, kv_loc, head_dim)
        q_rot = apply_rope(rms_scale(q_raw, q_gain), tok_pos).astype(jnp.bfloat16).reshape(n_steps, n_batch, kv_loc, groups, head_dim)
        k_new = apply_rope(rms_scale(k_raw, k_gain), tok_pos).astype(jnp.bfloat16).reshape(n_steps, n_batch, kv_loc, head_dim)
        new_keys, new_vals = k_new, v_new
        old_mask = (blk_pos[None, :] < start_pos[:, None])[:, None, None, None, :]
        step_ids = jnp.arange(n_steps)
        owned = (start_pos[:, None] + step_ids[None, :]) // seq_blk == lax.axis_index('sp')
        new_mask = (owned[:, None, :] & (step_ids[None, :] <= step_ids[:, None])[None])[:, None, :, None, :]
        old_scores = jnp.einsum('ibkgh,bskh->bkigs', q_rot, k_cache, preferred_element_type=jnp.float32) * score_scale
        old_scores = jnp.where(old_mask, old_scores, NEG_BIG)
        new_scores = jnp.einsum('ibkgh,jbkh->bkigj', q_rot, k_new, preferred_element_type=jnp.float32) * score_scale
        new_scores = jnp.where(new_mask, new_scores, NEG_BIG)
        blk_max = jnp.maximum(old_scores.max(axis=-1), new_scores.max(axis=-1))
        old_probs = jnp.where(old_mask, jnp.exp(old_scores - blk_max[..., None]), 0.0)
        new_probs = jnp.where(new_mask, jnp.exp(new_scores - blk_max[..., None]), 0.0)
        blk_sum = old_probs.sum(axis=-1) + new_probs.sum(axis=-1)
        blk_out = (jnp.einsum('bkigs,bskh->bkigh', old_probs.astype(jnp.bfloat16), v_cache, preferred_element_type=jnp.float32)
                   + jnp.einsum('bkigj,jbkh->bkigh', new_probs.astype(jnp.bfloat16), v_new, preferred_element_type=jnp.float32))
        top_max = lax.pmax(blk_max, 'sp')
        weights = jnp.exp(blk_max - top_max)
        packed = jnp.concatenate([blk_out * weights[..., None], (blk_sum * weights)[..., None]], axis=-1)
        summed = lax.psum(packed, 'sp')
        attn_vals = summed[..., :head_dim] / summed[..., head_dim:]
        attn_in = attn_vals.transpose(2, 0, 1, 3, 4).reshape(n_tok, heads_loc * head_dim).astype(jnp.bfloat16)
        attn_out = lax.psum(jnp.dot(attn_in, w_o, preferred_element_type=jnp.float32), 'tp')
        residual = (x_tok.astype(jnp.float32) + attn_out).astype(jnp.bfloat16)
        mlp_in = rms_scale(residual, mlp_norm).astype(jnp.bfloat16)
        gate_act = jnp.dot(mlp_in, w_gate, preferred_element_type=jnp.float32)
        up_proj = jnp.dot(mlp_in, w_up, preferred_element_type=jnp.float32)
        mlp_act = (jax.nn.silu(gate_act) * up_proj).astype(jnp.bfloat16)
        down_sum = lax.psum(jnp.dot(mlp_act, w_down, preferred_element_type=jnp.float32), 'tp')
        outputs = (residual.astype(jnp.float32) + down_sum).astype(jnp.bfloat16)
        offsets = blk_pos[None, :] - start_pos[:, None]
        k_out = k_cache
        v_out = v_cache
        for step_idx in range(n_steps):
            hit = (offsets == step_idx)[:, :, None, None]
            k_out = jnp.where(hit, new_keys[step_idx][:, None], k_out)
            v_out = jnp.where(hit, new_vals[step_idx][:, None], v_out)
        return outputs.reshape(hidden.shape), k_out, v_out

    return jax.shard_map(shard_body, mesh=mesh, in_specs=in_specs, out_specs=out_specs, check_vma=False)
```

time: 475 us -> 328 us (0.69)
  matrix products: 121 us -> 41.8 us
  other arithmetic: 140 us -> 101 us
  waiting for transfers between devices: 87.8 us -> 126 us
  local copies, waits for them, and re-layouts: 60.3 us -> 28.2 us
  blocking collectives: 42.4 us -> 13.2 us
    all_gather x4 -> x0, blocking collectives: 42.4 us -> none  [shard_body(): gathered = lax.all_gather(packed, 'sp')]
    psum x0 -> x1, waiting for transfers between devices: none -> 37.4 us  [shard_body(): summed = lax.psum(packed, 'sp')]
    dot_general x15 -> x4, matrix products: 43.1 us -> 18.3 us  [the longest x1 7.17 us: shard_body(): jnp.einsum('ibkgh,bskh->bkigs', q_rot, k_cache, preferred_element_type=jn...]
    dot_general x4 -> x1, matrix products: 31.1 us -> 9.91 us  [shard_body(): jnp.dot(mlp_act, w_down, preferred_element_type=jnp.float32)]
    unnamed x152 -> x48, local copies, waits for them, and re-layouts: 22.2 us -> 4.35 us
    another operation x22 -> x2, other arithmetic: 14.2 us -> 0.12 us
    pmax x0 -> x1, blocking collectives: none -> 13.2 us  [shard_body(): top_max = lax.pmax(blk_max, 'sp')]
    dot_general x4 -> x1, matrix products: 16.4 us -> 6.14 us  [shard_body(): gate_act = jnp.dot(mlp_in, w_gate, preferred_element_type=jnp.float32)]
  transfers between devices with their start and end apart: 2 -> 3, of which waited for: 2 -> 3; matrix products, arithmetic and copies ran while one was open for 18% -> 25% of each run, Pallas kernels for 0% -> 0%
where the time goes in v1:
time: 328 us; the launch traced here: 325 us
  waiting for transfers between devices  126 us (38%)
  other arithmetic  101 us (31%)
  matrix products  41.8 us (13%)
  local copies, waits for them, and re-layouts  28.2 us (9%)
  between operations  14.1 us (4%)
  blocking collectives  13.2 us (4%)
    psum x1, waiting for transfers between devices, shard_body(): lax.psum(jnp.dot(attn_in, w_o, preferred_element_type=jnp.float32), 'tp')  82.3 us
    select_n x1, other arithmetic, shard_body(): v_out = jnp.where(hit, new_vals[step_idx][:, None], v_out)  77.8 us
    psum x1, waiting for transfers between devices, shard_body(): summed = lax.psum(packed, 'sp')  37.4 us
    pmax x1, blocking collectives, shard_body(): top_max = lax.pmax(blk_max, 'sp')  13.2 us
    dot_general x1, matrix products, shard_body(): jnp.dot(mlp_act, w_down, preferred_element_type=jnp.float32)  9.91 us
    dot_general x1, matrix products, shard_body(): jnp.einsum('ibkgh,bskh->bkigs', q_rot, k_cache, preferred_element_type=jn...  7.17 us
    psum x1, waiting for transfers between devices, shard_body(): lax.psum(jnp.dot(mlp_act, w_down, preferred_element_type=jnp.float32), 'tp')  6.57 us
  transfers between devices with their start and end apart: 3, of which 3 were waited for; matrix products, arithmetic and copies ran while one was open for 25% of the time, Pallas kernels for 0%

profile of v1, /device:TPU:1, one launch (start us, length us, event | category | flops | bytes accessed | tf_op | source)
XLA Modules:
  0.0 325.3 jit_solution(9994251223533254540)
XLA Ops:
  7.2 0.5 iota_compare_fusion
  7.7 0.7 add_convert_fusion.2
  8.5 1.3 fusion.46
  9.7 0.7 convert_element_type.88
  10.4 0.7 convert_element_type.91
  11.1 1.5 fusion.9
  12.7 0.7 convert_element_type.85
  13.4 1.4 subtract_compare_fusion
  14.8 1.5 fusion.11
  16.4 2.3 copy.102
  18.6 1.7 multiply_reduce_fusion.1
  20.3 0.3 multiply_cosine_fusion
  20.8 0.1 concatenate.27
  20.9 0.8 copy.77
  21.8 0.8 copy.78
  22.6 3.9 %copy.99 = bf16[512,2048]{1,0:T(8,128)(2,1)} copy(bf16[512,2048]{0,1:T(8,128)(2,1)} %bitcast.56) | data formatting | bytes 4194304 | tf_op jit(solution)/shard_map/dot_general | solution.py:49
  26.5 2.3 multiply_reduce_fusion
  29.1 0.2 concatenate.24
  29.3 0.3 copy.73
  29.6 0.2 concatenate.25
  29.8 0.3 copy.74
  30.0 0.2 copy-done.8
  30.3 3.5 %fusion.35 = f32[64,2,4,2,4]{2,4,3,1,0:T(4,128)S(1)} fusion(bf16[4,64,2,64]{3,0,2,1:T(4,128)(2,1)} %copy.78, bf16[4,64,2,64]{3,0,2,1:T(4,128)(2,1)} %copy.77, bf16[4,64,2,2,64]{4,0,3,2,1:T(4,128)(2,1)S(1)} %copy.74, bf16[4,64,2,2,64]{4,0,3,2,1:T(4,128)(2,1)S(1)} %copy.73), kind=kOutput, calls=%fused_computation.66 | convolution fusion | flops 1835008 | bytes 409600 | tf_op jit(solution)/shard_map/ibkgh,jbkh->bkigj/dot_general | solution.py:61
  33.8 0.3 copy.79
  34.3 0.2 copy.109
  34.5 0.3 copy-done.7
  34.8 7.2 %fusion.54 = (f32[64,2,4,2]{2,3,1,0:T(2,128)S(1)}, f32[64,2,4,2,256]{4,2,3,1,0:T(4,128)}) fusion(bf16[64,256,2,128,1]{3,2,1,0,4:T(2,128)(2,1)} %bitcast.51, bf16[4,64,2,2,64]{4,0,3,2,1:T(4,128)(2,1)} %copy-done.9, bf16[4,64,2,2,64]{4,0,3,2,1:T(4,128)(2,1)} %copy-done.8, pred[64,256]{1,0:T(8,128)(4,1)S(1)} %copy-done.18), kind=kOutput, calls=%fused_computation.109 | convolution fusion | flops 68418560 | bytes 9719808 | tf_op jit(solution)/shard_map/ibkgh,bskh->bkigs/dot_general | solution.py:59
  42.1 0.7 copy.82
  42.8 13.2 %pmax.7 = f32[64,2,4,2]{2,3,1,0:T(2,128)} all-reduce(f32[64,2,4,2]{2,3,1,0:T(2,128)S(1)} %max.9), channel_id=1, replica_groups=mesh['dp'=2,'tp'=4,'sp'=4] {'sp'}, use_global_device_ids=true, to_apply=%region_5.6 | all-reduce | flops 1024 | bytes 8192 | tf_op jit(solution)/shard_map/pmax | solution.py:69
  56.0 0.3 fusion.13
  56.3 0.9 copy-done.6
  57.2 0.4 convolution_convert_fusion
  57.7 0.7 reshape.372
  58.4 1.4 fusion.44
  59.8 1.5 copy.110
  61.2 2.6 fusion.22
  63.9 5.9 %fusion = f32[64,2,4,2,128]{4,2,3,1,0:T(4,128)} fusion(bf16[64,256,2,128,1]{3,2,1,0,4:T(2,128)(2,1)} %bitcast.52, f32[64,2,4,2,256]{4,2,3,1,0:T(4,128)} %get-tuple-element.33, f32[64,2,4,2]{2,3,1,0:T(2,128)S(1)} %max.9, pred[64,256]{1,0:T(8,128)(4,1)} %get-tuple-element.27), kind=kOutput, calls=%fused_computation.8 | convolution fusion | flops 67895296 | bytes 9981952 | tf_op jit(solution)/shard_map/bkigs,bskh->bkigh/dot_general | solution.py:67
  69.8 1.0 copy.83
  70.8 1.9 multiply_bitcast_fusion
  72.7 3.3 %copy.87 = f32[64,2,4,2,1]{4,2,3,1,0:T(4,128)} copy(f32[64,2,4,2,1]{2,3,1,0,4:T(2,128)} %get-tuple-element.5) | data formatting | bytes 8192 | tf_op jit(solution)/shard_map/broadcast_in_dim | solution.py:71
  76.0 1.7 fusion.18
  77.6 1.3 pad_maximum_fusion
  79.0 37.4 %all-reduce.4.cloned.1.call-done = f32[64,2,4,2,129]{4,2,3,1,0:T(4,128)} async-done(((f32[64,2,4,2,129]{4,2,3,1,0:T(4,128)}), f32[64,2,4,2,129]{4,2,3,1,0:T(4,128)}) %all-reduce.4.cloned.1.call-update) | async-done | bytes 528400 | tf_op jit(solution)/shard_map/psum | solution.py:72
  116.3 1.9 slice.69
  118.2 1.3 copy.88
  119.5 0.2 copy.89
  119.7 1.4 fusion.34
  121.0 0.9 copy.90
  122.0 1.8 convert_element_type.98
  123.7 3.0 fusion.55
  126.7 0.3 all-reduce.8.cloned.1.call-start
  127.0 0.4 copy-done.20
  127.4 0.6 broadcast_in_dim.177
  128.0 0.6 broadcast_in_dim.183
  128.6 0.6 broadcast_in_dim.181
  129.3 0.6 broadcast_in_dim.179
  130.4 82.3 %all-reduce.6.cloned.1.call-done = f32[256,2048]{1,0:T(8,128)} async-done(((f32[256,2048]{1,0:T(8,128)}), f32[256,2048]{1,0:T(8,128)}) %all-reduce.6.cloned.1.call-update) | async-done | bytes 2097168 | tf_op jit(solution)/shard_map/psum | solution.py:75
  212.7 2.0 fusion.5
  214.7 6.1 %fusion.32 = f32[256,1536]{1,0:T(8,128)} fusion(bf16[2048,1536]{1,0:T(8,128)(2,1)} %param.23, bf16[256,2048]{1,0:T(8,128)(2,1)S(1)} %get-tuple-element.4, f32[2048]{0:T(1024)S(1)} %convert_element_type.101, f32[256]{0:T(256)S(1)} %add_rsqrt_fusion.3), kind=kOutput, calls=%fused_computation.48 | convolution fusion | flops 1612709888 | bytes 8922112 | tf_op jit(solution)/shard_map/dot_general | solution.py:78
  220.8 9.9 %fusion.24 = f32[256,2048]{1,0:T(8,128)} fusion(bf16[1536,2048]{1,0:T(8,128)(2,1)} %param.25, bf16[2048,1536]{1,0:T(8,128)(2,1)} %param.24, f32[256,1536]{1,0:T(8,128)} %fusion.32, bf16[256,2048]{1,0:T(8,128)(2,1)S(1)} %get-tuple-element.4, f32[2048]{0:T(1024)S(1)} %convert_element_type.101, f32[256]{0:T(256)S(1)} %add_rsqrt_fusion.3), kind=kOutput, calls=%fused_computation.40 | convolution fusion | flops 3225681920 | bytes 17310720 | tf_op jit(solution)/shard_map/dot_general | solution.py:81
  230.8 0.7 copy-done.10
  231.6 77.8 %broadcast_select_fusion.6 = (bf16[64,256,2,128]{3,2,1,0:T(2,128)(2,1)}, bf16[64,256,2,128]{3,2,1,0:T(2,128)(2,1)}) fusion(pred[64,256]{1,0:T(8,128)(4,1)S(1)} %copy-done.15, pred[64,256]{1,0:T(8,128)(4,1)S(1)} %copy-done.17, pred[64,256]{1,0:T(8,128)(4,1)S(1)} %copy-done.16, bf16[64,256,2,128]{3,2,1,0:T(2,128)(2,1)} %param.18, ...), kind=kLoop, calls=%fused_computation.6 | loop fusion | flops 33554432 | bytes 33882112 | tf_op jit(solution)/shard_map/jit(_where)/select_n | solution.py:89
  309.3 6.6 %all-reduce.8.cloned.1.call-done = f32[256,2048]{1,0:T(8,128)} async-done(((f32[256,2048]{1,0:T(8,128)}), f32[256,2048]{1,0:T(8,128)}) %all-reduce.8.cloned.1.call-update) | async-done | bytes 2097168 | tf_op jit(solution)/shard_map/psum | solution.py:81
  315.9 2.8 fusion.8
  (69 shorter events, 1.7 us)
Async XLA Ops:
  7.2 116.5 %copy-start = (bf16[512,2048]{1,0:T(8,128)(2,1)S(1)}, bf16[512,2048]{1,0:T(8,128)(2,1)}, u32[]{:S(2)}) copy-start(bf16[512,2048]{1,0:T(8,128)(2,1)} %param.22) | copy-start | bytes 6291460
  7.2 109.2 %all-reduce.4.cloned.1.call-start = ((), (), s32[]{:S(2)}) async-start(), calls=%async_computation | async-start | bytes 2097152 | tf_op jit(solution)/shard_map/psum | solution.py:72
  29.1 5.1 %copy-start.21 = (pred[4,4]{1,0:T(4,128)(4,1)S(1)}, pred[4,4]{1,0:T(4,128)(4,1)}, u32[]{:S(2)}) copy-start(pred[4,4]{1,0:T(4,128)(4,1)} %iota_compare_fusion) | copy-start | bytes 52
  29.1 5.0 %copy-start.22 = (pred[64,4]{0,1:T(4,128)(4,1)S(1)}, pred[64,4]{0,1:T(4,128)(4,1)}, u32[]{:S(2)}) copy-start(pred[64,4]{0,1:T(4,128)(4,1)} %fusion.46) | copy-start | bytes 772
  29.1 5.7 %copy-start.18 = (pred[64,256]{1,0:T(8,128)(4,1)S(1)}, pred[64,256]{1,0:T(8,128)(4,1)}, u32[]{:S(2)}) copy-start(pred[64,256]{1,0:T(8,128)(4,1)} %get-tuple-element.27) | copy-start | bytes 49156
  29.6 0.7 copy-start.8
  30.3 4.2 %copy-start.9 = (bf16[4,64,2,2,64]{4,0,3,2,1:T(4,128)(2,1)}, bf16[4,64,2,2,64]{4,0,3,2,1:T(4,128)(2,1)S(1)}, u32[]{:S(2)}) copy-start(bf16[4,64,2,2,64]{4,0,3,2,1:T(4,128)(2,1)S(1)} %copy.74) | copy-start | bytes 393220
  34.2 0.6 copy-start.7
  34.2 0.6 copy-start.19
  34.8 21.2 %copy-start.2 = (bf16[4,64,2048]{2,1,0:T(8,128)(2,1)S(1)}, bf16[4,64,2048]{2,1,0:T(8,128)(2,1)}, u32[]{:S(2)}) copy-start(bf16[4,64,2048]{2,1,0:T(8,128)(2,1)} %param.15) | copy-start | bytes 3145732
  56.0 1.2 copy-start.6
  76.0 1.7 copy-start.5
  78.9 133.8 %all-reduce.6.cloned.1.call-start = ((), (), s32[]{:S(2)}) async-start(), calls=%async_computation.1 | async-start | bytes 4194304 | tf_op jit(solution)/shard_map/psum | solution.py:75
  126.7 0.7 copy-start.20
  126.7 189.2 %all-reduce.8.cloned.1.call-start = ((), (), s32[]{:S(2)}) async-start(), calls=%async_computation.2 | async-start | bytes 4194304 | tf_op jit(solution)/shard_map/psum | solution.py:81
  214.7 6.2 %copy-start.3 = (bf16[256,2048]{1,0:T(8,128)(2,1)}, bf16[256,2048]{1,0:T(8,128)(2,1)S(1)}, u32[]{:S(2)}) copy-start(bf16[256,2048]{1,0:T(8,128)(2,1)S(1)} %get-tuple-element.4) | copy-start | bytes 3145732
  230.7 0.8 copy-start.10
  230.7 0.8 copy-start.11
  230.7 0.8 copy-start.12
  230.7 0.8 copy-start.13
  230.7 0.8 copy-start.14
  230.8 0.8 copy-start.15
  230.8 0.8 copy-start.16
  230.8 0.8 copy-start.17
  231.6 84.3 %copy-start.4 = (bf16[256,2048]{1,0:T(8,128)(2,1)S(1)}, bf16[256,2048]{1,0:T(8,128)(2,1)}, u32[]{:S(2)}) copy-start(bf16[256,2048]{1,0:T(8,128)(2,1)} %copy-done.3) | copy-start | bytes 3145732
  231.6 87.2 %copy-start.1 = (bf16[512,2048]{1,0:T(8,128)(2,1)S(1)}, bf16[512,2048]{1,0:T(8,128)(2,1)}, u32[]{:S(2)}) copy-start(bf16[512,2048]{1,0:T(8,128)(2,1)} %param.22) | copy-start | bytes 6291460
Sparse Core Ops, SparseCore 0:
  79.0 37.2 all-reduce.3
  126.8 85.7 all-reduce.5
  230.9 84.9 all-reduce.7

commit v2 on v1

v2 whole, which is shorter than its diff:
```python
import functools
import jax
import jax.numpy as jnp
import numpy as np
from jax import lax
from jax.experimental import pallas as pl
from jax.experimental.pallas import tpu as pltpu
from jax.sharding import PartitionSpec as P

ROPE_BASE = 1000000.0
NORM_EPS = 1e-06
NEG_BIG = -1e30
HEAD = 128
CHUNK = 4


def gain_row(ref):
    g = ref[...].astype(jnp.float32)
    return jnp.concatenate([g[j:j + 1] for j in range(g.shape[0])], axis=1)


def attend_kernel(start_ref, hid_hbm, wq_hbm, wk_hbm, wv_hbm, kc_hbm, vc_hbm, an_ref, qg_ref, kg_ref, freq_ref,
                  o_ref, ml_ref, ko_hbm, vo_hbm,
                  hid, wq, wk, wv, kbuf, vbuf, nrm, raw, q_s, k_s, v_s, pos_s, ml_s, key_s,
                  w_sem, h_sem, kin_sem, vin_sem, kout_sem, vout_sem):
    n_steps, n_batch, width = hid.shape
    rows = kbuf.shape[1]
    seq_blk = rows // 2
    n_chunk = n_batch // CHUNK
    n_q = wq.shape[1] // HEAD
    n_kv = wk.shape[1] // HEAD
    blk_start = lax.axis_index('sp') * seq_blk
    scale = HEAD ** -0.5

    hid_cp = pltpu.make_async_copy(hid_hbm, hid, h_sem)
    hid_cp.start()
    w_cps = [pltpu.make_async_copy(a, b, w_sem.at[j]) for j, (a, b) in enumerate(((wq_hbm, wq), (wk_hbm, wk), (wv_hbm, wv)))]
    for cp in w_cps:
        cp.start()

    def kv_in(c):
        sl = pl.ds(c * CHUNK, CHUNK)
        return (pltpu.make_async_copy(kc_hbm.at[sl], kbuf.at[sl], kin_sem.at[c]),
                pltpu.make_async_copy(vc_hbm.at[sl], vbuf.at[sl], vin_sem.at[c]))

    def kv_out(c):
        sl = pl.ds(c * CHUNK, CHUNK)
        return (pltpu.make_async_copy(kbuf.at[sl], ko_hbm.at[sl], kout_sem.at[c]),
                pltpu.make_async_copy(vbuf.at[sl], vo_hbm.at[sl], vout_sem.at[c]))

    @pl.loop(0, n_chunk)
    def _(c):
        a, b = kv_in(c)
        a.start()
        b.start()

    @pl.loop(0, n_batch)
    def _(b):
        pos_s[pl.ds(b, 1), :] = jnp.full((1, HEAD), start_ref[b].astype(jnp.float32), jnp.float32)

    freq = freq_ref[0:1, :]
    sign = freq_ref[1:2, :]
    ang = pos_s[...] * freq
    cos0 = jnp.cos(ang)
    sin0 = jnp.sin(ang)

    r_id = lax.broadcasted_iota(jnp.int32, (16, rows), 0)
    c_id = lax.broadcasted_iota(jnp.int32, (16, rows), 1)
    same = ((r_id % 4) // 2) == (c_id % 2)
    key_s[...] = jnp.where(same, c_id // 2 - r_id // 4, 1 << 20)

    hid_cp.wait()
    gain = gain_row(an_ref)
    for i in range(n_steps):
        for h in range(0, n_batch, 32):
            x = hid[i, h:h + 32, :].astype(jnp.float32)
            inv = lax.rsqrt(jnp.mean(x * x, axis=-1, keepdims=True) + NORM_EPS)
            nrm[i * n_batch + h:i * n_batch + h + 32, :] = (x * inv * gain).astype(jnp.bfloat16)

    def rope(x, g, cos, sin):
        inv = lax.rsqrt(jnp.mean(x * x, axis=-1, keepdims=True) + NORM_EPS)
        y = x * inv * g
        return y * cos + pltpu.roll(y, HEAD // 2, 1) * sin

    tabs = []
    for i in range(n_steps):
        if i == 0:
            c, s = cos0, sin0
        else:
            ci, si = jnp.cos(freq * float(i)), jnp.sin(freq * float(i))
            c, s = cos0 * ci - sin0 * si, sin0 * ci + cos0 * si
        pos_s_c, pos_s_s = c, s * sign
        tabs.append((pos_s_c, pos_s_s))

    for cp in w_cps:
        cp.wait()
    qg = qg_ref[...].astype(jnp.float32)
    kg = kg_ref[...].astype(jnp.float32)
    nq = n_q * HEAD
    nk = n_kv * HEAD
    raw[:, :nq] = jnp.dot(nrm[...], wq[...], preferred_element_type=jnp.float32)
    raw[:, nq:nq + nk] = jnp.dot(nrm[...], wk[...], preferred_element_type=jnp.float32)
    raw[:, nq + nk:] = jnp.dot(nrm[...], wv[...], preferred_element_type=jnp.float32)
    for i in range(n_steps):
        rs = slice(i * n_batch, (i + 1) * n_batch)
        cos, sin = tabs[i]
        for h in range(n_q):
            q_s[pl.ds(i * n_q + h, n_batch, stride=n_steps * n_q), :] = rope(raw[rs, h * HEAD:(h + 1) * HEAD], qg, cos, sin)
        for h in range(n_kv):
            k_s[pl.ds(i * n_kv + h, n_batch, stride=n_steps * n_kv), :] = rope(
                raw[rs, nq + h * HEAD:nq + (h + 1) * HEAD], kg, cos, sin)
            v_s[pl.ds(i * n_kv + h, n_batch, stride=n_steps * n_kv), :] = raw[rs, nq + nk + h * HEAD:nq + nk + (h + 1) * HEAD]

    row32 = lax.broadcasted_iota(jnp.int32, (32, HEAD), 0)
    eye_r = lax.broadcasted_iota(jnp.int32, (16, HEAD), 0)
    eye_c = lax.broadcasted_iota(jnp.int32, (16, HEAD), 1)
    eye_m = eye_r == eye_c
    eye_l = eye_r + 16 == eye_c
    zero24 = jnp.zeros((24, HEAD), jnp.float32)

    @pl.loop(0, n_chunk)
    def _(c):
        a, b = kv_in(c)
        a.wait()
        b.wait()
        lps = []
        for u in range(CHUNK):
            bb = c * CHUNK + u
            lp = start_ref[bb] - blk_start
            lps.append(lp)
            base = jnp.clip((lp // 8) * 8, 0, seq_blk - 16)
            rel = (lp - base) * 2
            shift = jnp.bitwise_and(rel, 31)
            hit = (row32 >= rel) & (row32 < rel + 8)
            win = pl.ds(pl.multiple_of(base * 2, 16), 32)
            for src, dst in ((k_s, kbuf), (v_s, vbuf)):
                new = src[pl.ds(pl.multiple_of(bb * 8, 8), 8), :]
                new = pltpu.roll(jnp.concatenate([new, zero24], axis=0), shift, 0)
                old = dst[bb, win, :].astype(jnp.float32)
                dst[bb, win, :] = jnp.where(hit, new, old).astype(jnp.bfloat16)
        for u in range(CHUNK):
            bb = c * CHUNK + u
            q = q_s[pl.ds(pl.multiple_of(bb * 16, 16), 16), :].astype(jnp.bfloat16)
            s = lax.dot_general(q, kbuf[bb], (((1,), (1,)), ((), ())), preferred_element_type=jnp.float32) * scale
            valid = key_s[...] <= lps[u]
            s = jnp.where(valid, s, NEG_BIG)
            m = jnp.max(s, axis=-1, keepdims=True)
            p = jnp.where(valid, jnp.exp(s - m), 0.0)
            l = jnp.sum(p, axis=-1, keepdims=True)
            o = jnp.dot(p.astype(jnp.bfloat16), vbuf[bb], preferred_element_type=jnp.float32)
            o_ref[pl.ds(bb, 16, stride=n_batch), :] = o
            ml = jnp.where(eye_m, m, 0.0) + jnp.where(eye_l, l, 0.0)
            ml_s[pl.ds(bb, 1), :] = jnp.sum(ml, axis=0, keepdims=True)
        a, b = kv_out(c)
        a.start()
        b.start()

    for i in range(n_steps):
        ml = ml_s[...]
        ml_ref[i] = ml if i == 0 else pltpu.roll(ml, HEAD - 4 * i, 1)

    @pl.loop(0, n_chunk)
    def _(c):
        a, b = kv_out(c)
        a.wait()
        b.wait()


def attend(start_pos, hidden, w_q, w_k, w_v, k_cache, v_cache, attn_norm, q_gain, k_gain):
    n_steps, n_batch, width = hidden.shape
    rows = k_cache.shape[1]
    n_chunk = n_batch // CHUNK
    nq, nk = w_q.shape[1], w_k.shape[1]
    half = HEAD // 2
    f = ROPE_BASE ** (-(np.arange(half, dtype=np.float64) * (2.0 / HEAD)))
    freq = np.stack([np.concatenate([f, f]), np.concatenate([-np.ones(half), np.ones(half)])]).astype(np.float32)
    vm = pl.BlockSpec(memory_space=pltpu.VMEM)
    anyspec = pl.BlockSpec(memory_space=pltpu.HBM)
    return pl.pallas_call(
        attend_kernel,
        name='attend',
        out_shape=(jax.ShapeDtypeStruct((16 * n_batch, HEAD), jnp.float32),
                   jax.ShapeDtypeStruct((n_steps, n_batch, HEAD), jnp.float32),
                   jax.ShapeDtypeStruct(k_cache.shape, jnp.bfloat16),
                   jax.ShapeDtypeStruct(v_cache.shape, jnp.bfloat16)),
        in_specs=[pl.BlockSpec(memory_space=pltpu.SMEM)] + [anyspec] * 6 + [vm] * 4,
        out_specs=(vm, vm, anyspec, anyspec),
        scratch_shapes=[
            pltpu.VMEM(hidden.shape, jnp.bfloat16),
            pltpu.VMEM(w_q.shape, jnp.bfloat16),
            pltpu.VMEM(w_k.shape, jnp.bfloat16),
            pltpu.VMEM(w_v.shape, jnp.bfloat16),
            pltpu.VMEM(k_cache.shape, jnp.bfloat16),
            pltpu.VMEM(v_cache.shape, jnp.bfloat16),
            pltpu.VMEM((n_steps * n_batch, width), jnp.bfloat16),
            pltpu.VMEM((n_steps * n_batch, nq + 2 * nk), jnp.float32),
            pltpu.VMEM((n_batch * 16, HEAD), jnp.float32),
            pltpu.VMEM((n_batch * 8, HEAD), jnp.float32),
            pltpu.VMEM((n_batch * 8, HEAD), jnp.float32),
            pltpu.VMEM((n_batch, HEAD), jnp.float32),
            pltpu.VMEM((n_batch, HEAD), jnp.float32),
            pltpu.VMEM((16, rows), jnp.int32),
            pltpu.SemaphoreType.DMA((3,)),
            pltpu.SemaphoreType.DMA,
            pltpu.SemaphoreType.DMA((n_chunk,)),
            pltpu.SemaphoreType.DMA((n_chunk,)),
            pltpu.SemaphoreType.DMA((n_chunk,)),
            pltpu.SemaphoreType.DMA((n_chunk,)),
        ],
        compiler_params=pltpu.CompilerParams(vmem_limit_bytes=67043328),
        cost_estimate=pl.CostEstimate(flops=2 * 10 ** 9, bytes_accessed=40 * 10 ** 6, transcendentals=10 ** 6),
    )(start_pos, hidden, w_q, w_k, w_v, k_cache, v_cache, attn_norm.reshape(-1, HEAD), q_gain.reshape(1, -1), k_gain.reshape(1, -1), jnp.asarray(freq))


N_COL = 8
N_HALF = 2
LAG = 3
LAG_Y = 3


def layer_kernel(o_hbm, ml_hbm, hid_hbm, wo_hbm, wg_hbm, wu_hbm, wd_hbm, mn_ref, out_ref,
                 o_own, ml_own, oa, mla, om, mlm, oy, mly, own, ml_mine, attn, hid, wo, wg, wu, wd,
                 p1, e1, x1, r1, m_s, act, p2, e2, x2, ob, yb, pb, pf,
                 ld_sem, w_sem, a1_snd, a1_rcv, a2_snd, a2_rcv, es1, er1, xs1, xr1, ts1, tr1,
                 es2, er2, xs2, xr2, ts2, tr2, ps, pr, ys, yr, fs, fr):
    n_steps, n_batch, width = hid_hbm.shape
    n_half = n_batch // N_HALF
    n_col = width // N_COL
    n_piece = N_COL * N_HALF
    tp = lax.axis_index('tp')
    sp = lax.axis_index('sp')
    core = sp % 2
    row = sp // 2
    partner = {'sp': row * 2 + 1 - core}
    across = {'sp': (1 - row) * 2 + core}
    is_mid = (tp % 3) != 0
    is_end = (tp % 3) == 0
    to_mid = {'tp': (tp + 3) // 3}
    to_end = {'tp': (tp - 1) * 3}
    to_other = {'tp': 3 - tp}
    mesh_id = pl.DeviceIdType.MESH

    def remote(src, dst, ssem, rsem, dev):
        return pltpu.make_async_remote_copy(src_ref=src, dst_ref=dst, send_sem=ssem, recv_sem=rsem, device_id=dev, device_id_type=mesh_id)

    lds = [pltpu.make_async_copy(o_hbm, o_own, ld_sem.at[0]), pltpu.make_async_copy(ml_hbm, ml_own, ld_sem.at[1]),
           pltpu.make_async_copy(hid_hbm.at[sp], hid, ld_sem.at[2])]
    wts = [pltpu.make_async_copy(a, b, w_sem.at[j]) for j, (a, b) in enumerate(((wo_hbm, wo), (wg_hbm, wg), (wu_hbm, wu), (wd_hbm, wd)))]
    for cp in lds + wts:
        cp.start()

    barrier = pltpu.get_barrier_semaphore()
    for dev in (partner, across):
        pl.semaphore_signal(barrier, inc=1, device_id=dev, device_id_type=mesh_id)

    @pl.when(is_mid)
    def _():
        pl.semaphore_signal(barrier, inc=1, device_id=to_end, device_id_type=mesh_id)
        pl.semaphore_signal(barrier, inc=1, device_id=to_other, device_id_type=mesh_id)
        pl.semaphore_wait(barrier, 4)

    @pl.when(is_end)
    def _():
        pl.semaphore_signal(barrier, inc=1, device_id=to_mid, device_id_type=mesh_id)
        pl.semaphore_wait(barrier, 3)

    for cp in lds:
        cp.wait()
    a1 = []
    for q, jy in enumerate((1 - row, row)):
        step = jy * 2 + 1 - core
        a1.append((remote(ml_own.at[step], mla.at[q], a1_snd.at[2 * q], a1_rcv.at[2 * q], partner),
                   remote(o_own.at[pl.ds(step * 4, 4)], oa.at[q], a1_snd.at[2 * q + 1], a1_rcv.at[2 * q + 1], partner)))
        for cp in a1[-1]:
            cp.start()

    lane = lax.broadcasted_iota(jnp.int32, (n_half, HEAD), 1)

    def weigh(ma, mb):
        top = jnp.maximum(ma, mb)
        wa, wb = jnp.exp(ma - top), jnp.exp(mb - top)
        tot = pltpu.roll(ma, HEAD - 16, 1) * wa + pltpu.roll(mb, HEAD - 16, 1) * wb
        return top, wa, wb, tot

    def merge_core(q, step, dst, mldst):
        for cp in a1[q]:
            cp.wait()
        for h in range(N_HALF):
            rs = pl.ds(h * n_half, n_half)
            top, wa, wb, tot = weigh(ml_own[step, rs, :], mla[q, rs, :])
            mldst[h] = jnp.where(lane < 16, top, pltpu.roll(tot, 16, 1))
            for k in range(4):
                dst[h, k] = o_own[step * 4 + k, rs, :] * wa[:, k:k + 1] + oa[q, k, rs, :] * wb[:, k:k + 1]

    merge_core(0, (1 - row) * 2 + core, om, mlm)
    a2 = []
    for h in range(N_HALF):
        a2.append((remote(mlm.at[h], mly.at[h], a2_snd.at[2 * h], a2_rcv.at[2 * h], across),
                   remote(om.at[h], oy.at[h], a2_snd.at[2 * h + 1], a2_rcv.at[2 * h + 1], across)))
        for cp in a2[-1]:
            cp.start()
    merge_core(1, row * 2 + core, own, ml_mine)
    wts[0].wait()

    e1_cp = lambda t: remote(p1.at[t], e1.at[t], es1.at[t], er1.at[t], to_mid)
    x1_cp = lambda t: remote(p1.at[t], x1.at[t], xs1.at[t], xr1.at[t], to_other)
    t1_cp = lambda t: remote(r1.at[t], r1.at[t], ts1.at[t], tr1.at[t], to_end)
    e2_cp = lambda t: remote(p2.at[t], e2.at[t], es2.at[t], er2.at[t], to_mid)
    x2_cp = lambda t: remote(p2.at[t], x2.at[t], xs2.at[t], xr2.at[t], to_other)
    t2_cp = lambda t: remote(ob.at[t], ob.at[t], ts2.at[t], tr2.at[t], to_end)
    p_cp = lambda t: remote(ob.at[t], pb.at[t], ps.at[t], pr.at[t], partner)
    y_cp = lambda t: remote(ob.at[t], yb.at[t], ys.at[t], yr.at[t], across)
    f_cp = lambda t: remote(yb.at[t], pf.at[t], fs.at[t], fr.at[t], partner)

    for h in range(N_HALF):
        for cp in a2[h]:
            cp.wait()
        _, wa, wb, tot = weigh(ml_mine[h], mly[h])
        inv = 1.0 / tot
        for k in range(4):
            val = (own[h, k] * wa[:, k:k + 1] + oy[h, k] * wb[:, k:k + 1]) * inv[:, k:k + 1]
            attn[h, :, k * HEAD:(k + 1) * HEAD] = val.astype(jnp.bfloat16)

        @pl.loop(0, N_COL)
        def _(n):
            cs = pl.ds(pl.multiple_of(n * n_col, n_col), n_col)
            t = h * N_COL + n
            p1[t] = jnp.dot(attn[h], wo[:, cs], preferred_element_type=jnp.float32)

            @pl.when(is_end)
            def _():
                e1_cp(t).start()

    @pl.when(is_mid)
    def _():
        @pl.loop(0, n_piece + LAG)
        def _(s):
            @pl.when(s < n_piece)
            def _():
                e1_cp(s).wait_recv()
                p1[s] = p1[s] + e1[s]
                x1_cp(s).start()

            @pl.when(s >= LAG)
            def _():
                t = s - LAG
                h = t // N_COL
                rs = pl.ds(pl.multiple_of(h * n_half, n_half), n_half)
                cs = pl.ds(pl.multiple_of((t - h * N_COL) * n_col, n_col), n_col)
                x1_cp(t).wait_recv()
                r = hid[rs, cs].astype(jnp.float32) + (p1[t] + x1[t])
                r1[t] = r.astype(jnp.bfloat16).astype(jnp.float32)
                t1_cp(t).start()

    @pl.when(is_end)
    def _():
        @pl.loop(0, n_piece)
        def _(t):
            t1_cp(t).wait_recv()

    gain = gain_row(mn_ref)
    for h in range(N_HALF):
        sq = jnp.zeros((n_half, 1), jnp.float32)
        for n in range(N_COL):
            r = r1[h * N_COL + n]
            sq = sq + jnp.sum(r * r, axis=-1, keepdims=True)
        inv = lax.rsqrt(sq / width + NORM_EPS)
        for n in range(N_COL):
            m_s[h * n_half:(h + 1) * n_half, n * n_col:(n + 1) * n_col] = (
                r1[h * N_COL + n] * inv * gain[:, n * n_col:(n + 1) * n_col]).astype(jnp.bfloat16)

    wts[1].wait()
    wts[2].wait()
    ffn = wg.shape[1]
    blk = 512
    for n in range(ffn // blk):
        cs = slice(n * blk, (n + 1) * blk)
        g = jnp.dot(m_s[...], wg[:, cs], preferred_element_type=jnp.float32)
        u = jnp.dot(m_s[...], wu[:, cs], preferred_element_type=jnp.float32)
        act[:, cs] = (jax.nn.silu(g) * u).astype(jnp.bfloat16)

    wts[3].wait()

    @pl.loop(0, N_COL)
    def _(n):
        cs = pl.ds(pl.multiple_of(n * n_col, n_col), n_col)
        d = jnp.dot(act[...], wd[:, cs], preferred_element_type=jnp.float32)
        for h in range(N_HALF):
            t = n * N_HALF + h
            p2[t] = d[h * n_half:(h + 1) * n_half]

            @pl.when(is_end)
            def _():
                e2_cp(t).start()

    def share(t):
        p_cp(t).start()
        y_cp(t).start()

    def relay(t):
        y_cp(t).wait_recv()
        f_cp(t).start()

    @pl.when(is_mid)
    def _():
        @pl.loop(0, n_piece + LAG + LAG_Y)
        def _(s):
            @pl.when(s < n_piece)
            def _():
                e2_cp(s).wait_recv()
                p2[s] = p2[s] + e2[s]
                x2_cp(s).start()

            @pl.when((s >= LAG) & (s < n_piece + LAG))
            def _():
                t = s - LAG
                n = t // N_HALF
                h = t - n * N_HALF
                x2_cp(t).wait_recv()
                o = r1[h * N_COL + n] + (p2[t] + x2[t])
                ob[t] = o.astype(jnp.bfloat16).astype(jnp.float32)
                t2_cp(t).start()
                share(t)

            @pl.when(s >= LAG + LAG_Y)
            def _():
                relay(s - LAG - LAG_Y)

    @pl.when(is_end)
    def _():
        @pl.loop(0, n_piece + LAG_Y)
        def _(s):
            @pl.when(s < n_piece)
            def _():
                t2_cp(s).wait_recv()
                share(s)

            @pl.when(s >= LAG_Y)
            def _():
                relay(s - LAG_Y)

    @pl.loop(0, n_piece)
    def _(t):
        n = t // N_HALF
        rs = pl.ds(pl.multiple_of((t - n * N_HALF) * n_half, n_half), n_half)
        cs = pl.ds(pl.multiple_of(n * n_col, n_col), n_col)
        out_ref[sp, rs, cs] = ob[t].astype(jnp.bfloat16)
        out_ref[(1 - row) * 2 + core, rs, cs] = yb[t].astype(jnp.bfloat16)
        p_cp(t).wait_recv()
        out_ref[row * 2 + 1 - core, rs, cs] = pb[t].astype(jnp.bfloat16)
        f_cp(t).wait_recv()
        out_ref[(1 - row) * 2 + 1 - core, rs, cs] = pf[t].astype(jnp.bfloat16)
        p_cp(t).wait_send()
        y_cp(t).wait_send()
        f_cp(t).wait_send()

        @pl.when(is_mid)
        def _():
            x1_cp(t).wait_send()
            t1_cp(t).wait_send()
            x2_cp(t).wait_send()
            t2_cp(t).wait_send()

        @pl.when(is_end)
        def _():
            e1_cp(t).wait_send()
            e2_cp(t).wait_send()


def layer(o, ml, hidden, w_o, w_gate, w_up, w_down, mlp_norm):
    n_steps, n_batch, width = hidden.shape
    n_half = n_batch // N_HALF
    n_col = width // N_COL
    n_piece = N_COL * N_HALF
    vm = pl.BlockSpec(memory_space=pltpu.VMEM)
    anyspec = pl.BlockSpec(memory_space=pltpu.HBM)
    f32, bf16 = jnp.float32, jnp.bfloat16
    piece = pltpu.VMEM((n_piece, n_half, n_col), f32)
    dma = pltpu.SemaphoreType.DMA
    return pl.pallas_call(
        layer_kernel,
        name='layer',
        out_shape=jax.ShapeDtypeStruct(hidden.shape, bf16),
        in_specs=[anyspec] * 7 + [vm],
        out_specs=vm,
        scratch_shapes=[
            pltpu.VMEM((16, n_batch, HEAD), f32),
            pltpu.VMEM((4, n_batch, HEAD), f32),
            pltpu.VMEM((2, 4, n_batch, HEAD), f32),
            pltpu.VMEM((2, n_batch, HEAD), f32),
            pltpu.VMEM((N_HALF, 4, n_half, HEAD), f32),
            pltpu.VMEM((N_HALF, n_half, HEAD), f32),
            pltpu.VMEM((N_HALF, 4, n_half, HEAD), f32),
            pltpu.VMEM((N_HALF, n_half, HEAD), f32),
            pltpu.VMEM((N_HALF, 4, n_half, HEAD), f32),
            pltpu.VMEM((N_HALF, n_half, HEAD), f32),
            pltpu.VMEM((N_HALF, n_half, 4 * HEAD), bf16),
            pltpu.VMEM((n_batch, width), bf16),
            pltpu.VMEM(w_o.shape, bf16),
            pltpu.VMEM(w_gate.shape, bf16),
            pltpu.VMEM(w_up.shape, bf16),
            pltpu.VMEM(w_down.shape, bf16),
            piece, piece, piece, piece,
            pltpu.VMEM((n_batch, width), bf16),
            pltpu.VMEM((n_batch, w_gate.shape[1]), bf16),
            piece, piece, piece, piece, piece, piece, piece,
            dma((3,)), dma((4,)), dma((4,)), dma((4,)), dma((2 * N_HALF,)), dma((2 * N_HALF,)),
        ] + [dma((n_piece,))] * 18,
        compiler_params=pltpu.CompilerParams(collective_id=0, has_side_effects=True, vmem_limit_bytes=67043328),
        cost_estimate=pl.CostEstimate(flops=2 * 10 ** 9, bytes_accessed=30 * 10 ** 6, transcendentals=10 ** 6),
    )(o.reshape(16, n_batch, HEAD), ml, hidden, w_o, w_gate, w_up, w_down, mlp_norm.reshape(-1, HEAD))


def solution(mesh):
    cache_spec = P('dp', 'sp', 'tp', None)
    col_spec = P(None, 'tp')
    row_spec = P('tp', None)
    in_specs = (P(None, 'dp', None), P('dp'), cache_spec, cache_spec, col_spec, col_spec, col_spec, row_spec,
                col_spec, col_spec, row_spec, P(), P(), P(), P())
    out_specs = (P(None, 'dp', None), cache_spec, cache_spec)

    def shard_body(hidden, start_pos, k_cache, v_cache, w_q, w_k, w_v, w_o, w_gate, w_up, w_down, attn_norm, mlp_norm, q_gain, k_gain):
        flat = (k_cache.shape[0], k_cache.shape[1] * k_cache.shape[2], k_cache.shape[3])
        o, ml, k_out, v_out = attend(start_pos, hidden, w_q, w_k, w_v, k_cache.reshape(flat), v_cache.reshape(flat), attn_norm, q_gain, k_gain)
        out = layer(o, ml, hidden, w_o, w_gate, w_up, w_down, mlp_norm)
        return out, k_out.reshape(k_cache.shape), v_out.reshape(v_cache.shape)

    return jax.shard_map(shard_body, mesh=mesh, in_specs=in_specs, out_specs=out_specs, check_vma=False)
```

time: 328 us -> 95.5 us (0.29)
  waiting for transfers between devices: 126 us -> 0 us
  other arithmetic: 101 us -> 0 us
  Pallas kernels: 0 us -> 92.2 us
  matrix products: 41.8 us -> 0 us
  local copies, waits for them, and re-layouts: 28.2 us -> 2.3 us
  between operations: 14.1 us -> 0.65 us
  blocking collectives: 13.2 us -> 0 us
    psum x3 -> x0, waiting for transfers between devices: 126 us -> none  [the longest x1 82.3 us: shard_body(): lax.psum(jnp.dot(attn_in, w_o, preferred_element_type=jnp.float32), 'tp')]
    pallas_call x0 -> x2, Pallas kernels: none -> 92.2 us  [the longest x1 67.5 us: layer(): pl.pallas_call(layer_kernel, name='layer', out_shape=jax.ShapeDtypeStruct...]
    select_n x1 -> x0, other arithmetic: 77.8 us -> none  [shard_body(): v_out = jnp.where(hit, new_vals[step_idx][:, None], v_out)]
    dot_general x10 -> x0, matrix products: 41.8 us -> none  [the longest x1 9.91 us: shard_body(): jnp.dot(mlp_act, w_down, preferred_element_type=jnp.float32)]
    pmax x1 -> x0, blocking collectives: 13.2 us -> none  [shard_body(): top_max = lax.pmax(blk_max, 'sp')]
    convert_element_type x10 -> x0, other arithmetic: 10.2 us -> none  [the longest x1 2.85 us: shard_body(): outputs = (residual.astype(jnp.float32) + down_sum).astype(jnp.bfloat16)]
    dot_general x3 -> x0, local copies, waits for them, and re-layouts: 6.53 us -> none  [the longest x1 3.91 us: shard_body(): jnp.dot(normed, w_q, preferred_element_type=jnp.float32)]
    reduce_sum x3 -> x0, other arithmetic: 6.13 us -> none  [the longest x2 3.49 us: rms_scale(): jnp.mean(wide_vals * wide_vals, axis=-1, keepdims=True) + NORM_EPS]
  transfers between devices with their start and end apart: 3 -> 0, of which waited for: 3 -> 0; matrix products, arithmetic and copies ran while one was open for 25% -> 0% of each run, Pallas kernels for 0% -> 0%
where the time goes in v2:
time: 95.5 us; the launch traced here: 95.1 us
  Pallas kernels  92.2 us (97%)
  local copies, waits for them, and re-layouts  2.3 us (2%)
    pallas_call x1, Pallas kernels, layer(): pl.pallas_call(layer_kernel, name='layer', out_shape=jax.ShapeDtypeStruct...  67.5 us
    pallas_call x1, Pallas kernels, attend(): pl.pallas_call(attend_kernel, name='attend', out_shape=(jax.ShapeDtypeStr...  24.7 us
    unnamed x1, local copies, waits for them, and re-layouts  2.3 us

profile of v2, /device:TPU:1, one launch (start us, length us, event | category | flops | bytes accessed | tf_op | source)
XLA Modules:
  0.0 95.1 jit_solution(9586942301129164373)
XLA Ops:
  0.6 24.7 %attend.1 = (f32[1024,128]{1,0:T(8,128)}, f32[4,64,128]{2,1,0:T(8,128)}, bf16[64,512,128]{2,1,0:T(8,128)(2,1)}, bf16[64,512,128]{2,1,0:T(8,128)(2,1)}) custom-call(s32[64]{0:T(128)} %start_ref.1, bf16[4,64,2048]{2,1,0:T(8,128)(2,1)} %hid_hbm.3, bf16[2048,512]{1,0:T(8,128)(2,1)} %wq_hbm.1, bf16[2048,256]{1,0:T(8,128)(2,1)} %wk_hbm.1, ...), custom_call_target="tpu_custom_call" | custom-call | flops 2000000000 | bytes 40000000 | tf_op jit(solution)/shard_map/attend/pallas_call | solution.py:179
  25.3 67.5 %layer.1 = bf16[4,64,2048]{2,1,0:T(8,128)(2,1)} custom-call(f32[16,64,128]{2,1,0:T(8,128)} %bitcast.11, f32[4,64,128]{2,1,0:T(8,128)} %get-tuple-element.8.ml_hbm, bf16[4,64,2048]{2,1,0:T(8,128)(2,1)} %hid_hbm.3, bf16[512,2048]{1,0:T(8,128)(2,1)} %wo_hbm.1, bf16[2048,1536]{1,0:T(8,128)(2,1)} %wg_hbm.1, bf16[2048,1536]{1,0:T(8,128)(2,1)} %wu_hbm.1, ...), custom_call_target="tpu_custom_call" | custom-call | flops 2000000000 | bytes 30000000 | tf_op jit(solution)/shard_map/layer/pallas_call | solution.py:480
  92.8 2.3 %copy.20 = bf16[4,64,2048]{2,1,0:T(8,128)(2,1)} copy(bf16[4,64,2048]{2,1,0:T(8,128)(2,1)} %layer.1) | data formatting | bytes 2097152

commit v3 on v2

--- a/solution.py
+++ b/solution.py
@@ -11,7 +11,7 @@
 NORM_EPS = 1e-06
 NEG_BIG = -1e30
 HEAD = 128
-CHUNK = 4
+CHUNK = 8
 
 
 def gain_row(ref):
@@ -21,7 +21,7 @@
 
 def attend_kernel(start_ref, hid_hbm, wq_hbm, wk_hbm, wv_hbm, kc_hbm, vc_hbm, an_ref, qg_ref, kg_ref, freq_ref,
                   o_ref, ml_ref, ko_hbm, vo_hbm,
-                  hid, wq, wk, wv, kbuf, vbuf, nrm, raw, q_s, k_s, v_s, pos_s, ml_s, key_s,
+                  hid, wq, wk, wv, kbuf, vbuf, nrm, raw, q_s, k_s, v_s, pos_s, ml_s, key_s, sc_s, pr_s,
                   w_sem, h_sem, kin_sem, vin_sem, kout_sem, vout_sem):
     n_steps, n_batch, width = hid.shape
     rows = kbuf.shape[1]
@@ -141,16 +141,23 @@
         for u in range(CHUNK):
             bb = c * CHUNK + u
             q = q_s[pl.ds(pl.multiple_of(bb * 16, 16), 16), :].astype(jnp.bfloat16)
-            s = lax.dot_general(q, kbuf[bb], (((1,), (1,)), ((), ())), preferred_element_type=jnp.float32) * scale
-            valid = key_s[...] <= lps[u]
-            s = jnp.where(valid, s, NEG_BIG)
-            m = jnp.max(s, axis=-1, keepdims=True)
-            p = jnp.where(valid, jnp.exp(s - m), 0.0)
-            l = jnp.sum(p, axis=-1, keepdims=True)
-            o = jnp.dot(p.astype(jnp.bfloat16), vbuf[bb], preferred_element_type=jnp.float32)
-            o_ref[pl.ds(bb, 16, stride=n_batch), :] = o
-            ml = jnp.where(eye_m, m, 0.0) + jnp.where(eye_l, l, 0.0)
-            ml_s[pl.ds(bb, 1), :] = jnp.sum(ml, axis=0, keepdims=True)
+            sc_s[u] = lax.dot_general(q, kbuf[bb], (((1,), (1,)), ((), ())), preferred_element_type=jnp.float32)
+        tops = []
+        for u in range(CHUNK):
+            s = jnp.where(key_s[...] <= lps[u], sc_s[u] * scale, NEG_BIG)
+            sc_s[u] = s
+            tops.append(jnp.maximum(jnp.max(s, axis=-1, keepdims=True), 0.5 * NEG_BIG))
+        sums = []
+        for u in range(CHUNK):
+            p = jnp.exp(sc_s[u] - tops[u])
+            sums.append(jnp.sum(p, axis=-1, keepdims=True))
+            pr_s[u] = p.astype(jnp.bfloat16)
+        for u in range(CHUNK):
+            bb = c * CHUNK + u
+            o_ref[pl.ds(bb, 16, stride=n_batch), :] = jnp.dot(pr_s[u], vbuf[bb], preferred_element_type=jnp.float32)
+        for u in range(CHUNK):
+            ml = jnp.where(eye_m, tops[u], 0.0) + jnp.where(eye_l, sums[u], 0.0)
+            ml_s[pl.ds(c * CHUNK + u, 1), :] = jnp.sum(ml, axis=0, keepdims=True)
         a, b = kv_out(c)
         a.start()
         b.start()
@@ -200,6 +207,8 @@
             pltpu.VMEM((n_batch, HEAD), jnp.float32),
             pltpu.VMEM((n_batch, HEAD), jnp.float32),
             pltpu.VMEM((16, rows), jnp.int32),
+            pltpu.VMEM((CHUNK, 16, rows), jnp.float32),
+            pltpu.VMEM((CHUNK, 16, rows), jnp.bfloat16),
             pltpu.SemaphoreType.DMA((3,)),
             pltpu.SemaphoreType.DMA,
             pltpu.SemaphoreType.DMA((n_chunk,)),
@@ -214,12 +223,12 @@
 
 N_COL = 8
 N_HALF = 2
-LAG = 3
-LAG_Y = 3
-
-
-def layer_kernel(o_hbm, ml_hbm, hid_hbm, wo_hbm, wg_hbm, wu_hbm, wd_hbm, mn_ref, out_ref,
-                 o_own, ml_own, oa, mla, om, mlm, oy, mly, own, ml_mine, attn, hid, wo, wg, wu, wd,
+LAG = 5
+LAG_Y = 8
+
+
+def layer_kernel(o_own, ml_own, hid_hbm, wo_hbm, wg_hbm, wu_hbm, wd_hbm, mn_ref, out_ref,
+                 oa, mla, om, mlm, oy, mly, own, ml_mine, attn, hid, wo, wg, wu, wd,
                  p1, e1, x1, r1, m_s, act, p2, e2, x2, ob, yb, pb, pf,
                  ld_sem, w_sem, a1_snd, a1_rcv, a2_snd, a2_rcv, es1, er1, xs1, xr1, ts1, tr1,
                  es2, er2, xs2, xr2, ts2, tr2, ps, pr, ys, yr, fs, fr):
@@ -243,10 +252,9 @@
     def remote(src, dst, ssem, rsem, dev):
         return pltpu.make_async_remote_copy(src_ref=src, dst_ref=dst, send_sem=ssem, recv_sem=rsem, device_id=dev, device_id_type=mesh_id)
 
-    lds = [pltpu.make_async_copy(o_hbm, o_own, ld_sem.at[0]), pltpu.make_async_copy(ml_hbm, ml_own, ld_sem.at[1]),
-           pltpu.make_async_copy(hid_hbm.at[sp], hid, ld_sem.at[2])]
+    lds = [pltpu.make_async_copy(hid_hbm.at[sp], hid, ld_sem)]
     wts = [pltpu.make_async_copy(a, b, w_sem.at[j]) for j, (a, b) in enumerate(((wo_hbm, wo), (wg_hbm, wg), (wu_hbm, wu), (wd_hbm, wd)))]
-    for cp in lds + wts:
+    for cp in lds:
         cp.start()
 
     barrier = pltpu.get_barrier_semaphore()
@@ -299,6 +307,8 @@
                    remote(om.at[h], oy.at[h], a2_snd.at[2 * h + 1], a2_rcv.at[2 * h + 1], across)))
         for cp in a2[-1]:
             cp.start()
+    for cp in wts:
+        cp.start()
     merge_core(1, row * 2 + core, own, ml_mine)
     wts[0].wait()
 
@@ -312,6 +322,20 @@
     y_cp = lambda t: remote(ob.at[t], yb.at[t], ys.at[t], yr.at[t], across)
     f_cp = lambda t: remote(yb.at[t], pf.at[t], fs.at[t], fr.at[t], partner)
 
+    def spread(h, lhs, w, dst, cp):
+        wide = width // 2
+        per = N_COL // 2
+        for j in range(2):
+            d = jnp.dot(lhs, w[:, j * wide:(j + 1) * wide], preferred_element_type=jnp.float32)
+            for n in range(per):
+                dst[h * N_COL + j * per + n] = d[:, n * n_col:(n + 1) * n_col]
+
+            @pl.when(is_end)
+            def _():
+                @pl.loop(h * N_COL + j * per, h * N_COL + (j + 1) * per)
+                def _(t):
+                    cp(t).start()
+
     for h in range(N_HALF):
         for cp in a2[h]:
             cp.wait()
@@ -321,77 +345,68 @@
             val = (own[h, k] * wa[:, k:k + 1] + oy[h, k] * wb[:, k:k + 1]) * inv[:, k:k + 1]
             attn[h, :, k * HEAD:(k + 1) * HEAD] = val.astype(jnp.bfloat16)
 
-        @pl.loop(0, N_COL)
-        def _(n):
-            cs = pl.ds(pl.multiple_of(n * n_col, n_col), n_col)
-            t = h * N_COL + n
-            p1[t] = jnp.dot(attn[h], wo[:, cs], preferred_element_type=jnp.float32)
-
-            @pl.when(is_end)
-            def _():
-                e1_cp(t).start()
-
-    @pl.when(is_mid)
-    def _():
-        @pl.loop(0, n_piece + LAG)
-        def _(s):
-            @pl.when(s < n_piece)
-            def _():
-                e1_cp(s).wait_recv()
-                p1[s] = p1[s] + e1[s]
-                x1_cp(s).start()
-
-            @pl.when(s >= LAG)
-            def _():
-                t = s - LAG
-                h = t // N_COL
-                rs = pl.ds(pl.multiple_of(h * n_half, n_half), n_half)
-                cs = pl.ds(pl.multiple_of((t - h * N_COL) * n_col, n_col), n_col)
-                x1_cp(t).wait_recv()
-                r = hid[rs, cs].astype(jnp.float32) + (p1[t] + x1[t])
-                r1[t] = r.astype(jnp.bfloat16).astype(jnp.float32)
-                t1_cp(t).start()
-
-    @pl.when(is_end)
-    def _():
-        @pl.loop(0, n_piece)
-        def _(t):
-            t1_cp(t).wait_recv()
+        spread(h, attn[h], wo, p1, e1_cp)
+
+    def sum_step(s):
+        @pl.when(s < n_piece)
+        def _():
+            e1_cp(s).wait_recv()
+            p1[s] = p1[s] + e1[s]
+            x1_cp(s).start()
+
+        @pl.when(s >= LAG)
+        def _():
+            t = s - LAG
+            h = t // N_COL
+            rs = pl.ds(pl.multiple_of(h * n_half, n_half), n_half)
+            cs = pl.ds(pl.multiple_of((t - h * N_COL) * n_col, n_col), n_col)
+            x1_cp(t).wait_recv()
+            r = hid[rs, cs].astype(jnp.float32) + (p1[t] + x1[t])
+            r1[t] = r.astype(jnp.bfloat16).astype(jnp.float32)
+            t1_cp(t).start()
+
+    def sum_steps(lo, hi):
+        @pl.when(is_mid)
+        def _():
+            pl.loop(lo, hi)(sum_step)
+
+    def end_recv(lo, hi):
+        @pl.when(is_end)
+        def _():
+            @pl.loop(lo, hi)
+            def _(t):
+                t1_cp(t).wait_recv()
 
     gain = gain_row(mn_ref)
+    ffn = wg.shape[1]
+    blk = ffn // 3
+    done = 0
     for h in range(N_HALF):
+        stop = (h + 1) * N_COL + LAG
+        sum_steps(done, stop)
+        done = stop
+        end_recv(h * N_COL, (h + 1) * N_COL)
         sq = jnp.zeros((n_half, 1), jnp.float32)
         for n in range(N_COL):
             r = r1[h * N_COL + n]
             sq = sq + jnp.sum(r * r, axis=-1, keepdims=True)
         inv = lax.rsqrt(sq / width + NORM_EPS)
         for n in range(N_COL):
-            m_s[h * n_half:(h + 1) * n_half, n * n_col:(n + 1) * n_col] = (
-                r1[h * N_COL + n] * inv * gain[:, n * n_col:(n + 1) * n_col]).astype(jnp.bfloat16)
-
-    wts[1].wait()
-    wts[2].wait()
-    ffn = wg.shape[1]
-    blk = 512
-    for n in range(ffn // blk):
-        cs = slice(n * blk, (n + 1) * blk)
-        g = jnp.dot(m_s[...], wg[:, cs], preferred_element_type=jnp.float32)
-        u = jnp.dot(m_s[...], wu[:, cs], preferred_element_type=jnp.float32)
-        act[:, cs] = (jax.nn.silu(g) * u).astype(jnp.bfloat16)
-
-    wts[3].wait()
-
-    @pl.loop(0, N_COL)
-    def _(n):
-        cs = pl.ds(pl.multiple_of(n * n_col, n_col), n_col)
-        d = jnp.dot(act[...], wd[:, cs], preferred_element_type=jnp.float32)
-        for h in range(N_HALF):
-            t = n * N_HALF + h
-            p2[t] = d[h * n_half:(h + 1) * n_half]
-
-            @pl.when(is_end)
-            def _():
-                e2_cp(t).start()
+            m_s[:, n * n_col:(n + 1) * n_col] = (r1[h * N_COL + n] * inv * gain[:, n * n_col:(n + 1) * n_col]).astype(jnp.bfloat16)
+        if h == 0:
+            wts[1].wait()
+            wts[2].wait()
+        for n in range(3):
+            cs = slice(n * blk, (n + 1) * blk)
+            g = jnp.dot(m_s[...], wg[:, cs], preferred_element_type=jnp.float32)
+            u = jnp.dot(m_s[...], wu[:, cs], preferred_element_type=jnp.float32)
+            act[:, cs] = (jax.nn.silu(g) * u).astype(jnp.bfloat16)
+            if h + 1 < N_HALF:
+                sum_steps(done, done + 2)
+                done += 2
+        if h == 0:
+            wts[3].wait()
+        spread(h, act[...], wd, p2, e2_cp)
 
     def share(t):
         p_cp(t).start()
@@ -414,10 +429,8 @@
             @pl.when((s >= LAG) & (s < n_piece + LAG))
             def _():
                 t = s - LAG
-                n = t // N_HALF
-                h = t - n * N_HALF
                 x2_cp(t).wait_recv()
-                o = r1[h * N_COL + n] + (p2[t] + x2[t])
+                o = r1[t] + (p2[t] + x2[t])
                 ob[t] = o.astype(jnp.bfloat16).astype(jnp.float32)
                 t2_cp(t).start()
                 share(t)
@@ -441,9 +454,9 @@
 
     @pl.loop(0, n_piece)
     def _(t):
-        n = t // N_HALF
-        rs = pl.ds(pl.multiple_of((t - n * N_HALF) * n_half, n_half), n_half)
-        cs = pl.ds(pl.multiple_of(n * n_col, n_col), n_col)
+        h = t // N_COL
+        rs = pl.ds(pl.multiple_of(h * n_half, n_half), n_half)
+        cs = pl.ds(pl.multiple_of((t - h * N_COL) * n_col, n_col), n_col)
         out_ref[sp, rs, cs] = ob[t].astype(jnp.bfloat16)
         out_ref[(1 - row) * 2 + core, rs, cs] = yb[t].astype(jnp.bfloat16)
         p_cp(t).wait_recv()
@@ -481,11 +494,9 @@
         layer_kernel,
         name='layer',
         out_shape=jax.ShapeDtypeStruct(hidden.shape, bf16),
-        in_specs=[anyspec] * 7 + [vm],
+        in_specs=[vm] * 2 + [anyspec] * 5 + [vm],
         out_specs=vm,
         scratch_shapes=[
-            pltpu.VMEM((16, n_batch, HEAD), f32),
-            pltpu.VMEM((4, n_batch, HEAD), f32),
             pltpu.VMEM((2, 4, n_batch, HEAD), f32),
             pltpu.VMEM((2, n_batch, HEAD), f32),
             pltpu.VMEM((N_HALF, 4, n_half, HEAD), f32),
@@ -501,10 +512,10 @@
             pltpu.VMEM(w_up.shape, bf16),
             pltpu.VMEM(w_down.shape, bf16),
             piece, piece, piece, piece,
-            pltpu.VMEM((n_batch, width), bf16),
-            pltpu.VMEM((n_batch, w_gate.shape[1]), bf16),
+            pltpu.VMEM((n_half, width), bf16),
+            pltpu.VMEM((n_half, w_gate.shape[1]), bf16),
             piece, piece, piece, piece, piece, piece, piece,
-            dma((3,)), dma((4,)), dma((4,)), dma((4,)), dma((2 * N_HALF,)), dma((2 * N_HALF,)),
+            dma, dma((4,)), dma((4,)), dma((4,)), dma((2 * N_HALF,)), dma((2 * N_HALF,)),
         ] + [dma((n_piece,))] * 18,
         compiler_params=pltpu.CompilerParams(collective_id=0, has_side_effects=True, vmem_limit_bytes=67043328),
         cost_estimate=pl.CostEstimate(flops=2 * 10 ** 9, bytes_accessed=30 * 10 ** 6, transcendentals=10 ** 6),

time: 95.5 us -> 73.4 us (0.77)
  Pallas kernels: 92.2 us -> 70.1 us
    pallas_call x1, Pallas kernels: 67.5 us -> 54.8 us  [layer(): pl.pallas_call(layer_kernel, name='layer', out_shape=jax.ShapeDtypeStruct...]
    pallas_call x1, Pallas kernels: 24.7 us -> 15.3 us  [attend(): pl.pallas_call(attend_kernel, name='attend', out_shape=(jax.ShapeDtypeStr...]
where the time goes in v3:
time: 73.4 us; the launch traced here: 73 us
  Pallas kernels  70.1 us (96%)
  local copies, waits for them, and re-layouts  2.3 us (3%)
    pallas_call x1, Pallas kernels, layer(): pl.pallas_call(layer_kernel, name='layer', out_shape=jax.ShapeDtypeStruct...  54.8 us
    pallas_call x1, Pallas kernels, attend(): pl.pallas_call(attend_kernel, name='attend', out_shape=(jax.ShapeDtypeStr...  15.3 us
    unnamed x1, local copies, waits for them, and re-layouts  2.3 us

profile of v3, /device:TPU:1, one launch (start us, length us, event | category | flops | bytes accessed | tf_op | source)
XLA Modules:
  0.0 73.0 jit_solution(363762294846685585)
XLA Ops:
  0.6 15.3 %attend.1 = (f32[1024,128]{1,0:T(8,128)}, f32[4,64,128]{2,1,0:T(8,128)}, bf16[64,512,128]{2,1,0:T(8,128)(2,1)}, bf16[64,512,128]{2,1,0:T(8,128)(2,1)}) custom-call(s32[64]{0:T(128)} %start_ref.1, bf16[4,64,2048]{2,1,0:T(8,128)(2,1)} %hid_hbm.3, bf16[2048,512]{1,0:T(8,128)(2,1)} %wq_hbm.1, bf16[2048,256]{1,0:T(8,128)(2,1)} %wk_hbm.1, ...), custom_call_target="tpu_custom_call" | custom-call | flops 2000000000 | bytes 40000000 | tf_op jit(solution)/shard_map/attend/pallas_call | solution.py:186
  15.9 54.8 %layer.1 = bf16[4,64,2048]{2,1,0:T(8,128)(2,1)} custom-call(f32[16,64,128]{2,1,0:T(8,128)} %bitcast.11, f32[4,64,128]{2,1,0:T(8,128)} %get-tuple-element.8.ml_own, bf16[4,64,2048]{2,1,0:T(8,128)(2,1)} %hid_hbm.3, bf16[512,2048]{1,0:T(8,128)(2,1)} %wo_hbm.1, bf16[2048,1536]{1,0:T(8,128)(2,1)} %wg_hbm.1, bf16[2048,1536]{1,0:T(8,128)(2,1)} %wu_hbm.1, ...), custom_call_target="tpu_custom_call" | custom-call | flops 2000000000 | bytes 30000000 | tf_op jit(solution)/shard_map/layer/pallas_call | solution.py:493
  70.7 2.3 %copy.20 = bf16[4,64,2048]{2,1,0:T(8,128)(2,1)} copy(bf16[4,64,2048]{2,1,0:T(8,128)(2,1)} %layer.1) | data formatting | bytes 2097152

commit v4 on v3

--- a/solution.py
+++ b/solution.py
@@ -221,16 +221,18 @@
     )(start_pos, hidden, w_q, w_k, w_v, k_cache, v_cache, attn_norm.reshape(-1, HEAD), q_gain.reshape(1, -1), k_gain.reshape(1, -1), jnp.asarray(freq))
 
 
-N_COL = 8
-N_HALF = 2
+N_COL = 4
+N_HALF = 4
 LAG = 5
 LAG_Y = 8
-
-
-def layer_kernel(o_own, ml_own, hid_hbm, wo_hbm, wg_hbm, wu_hbm, wd_hbm, mn_ref, out_ref,
-                 oa, mla, om, mlm, oy, mly, own, ml_mine, attn, hid, wo, wg, wu, wd,
+TILES = 3
+SERVE = 1
+
+
+def layer_kernel(o_hbm, ml_hbm, hid_hbm, wo_hbm, wg_hbm, wu_hbm, wd_hbm, mn_hbm, out_hbm,
+                 o_own, ml_own, mn_ref, out_ref, oa, mla, om, mlm, oy, mly, own, ml_mine, attn, hid, wo, wg, wu, wd,
                  p1, e1, x1, r1, m_s, act, p2, e2, x2, ob, yb, pb, pf,
-                 ld_sem, w_sem, a1_snd, a1_rcv, a2_snd, a2_rcv, es1, er1, xs1, xr1, ts1, tr1,
+                 ld_sem, out_sem, w_sem, a1_snd, a1_rcv, a2_snd, a2_rcv, es1, er1, xs1, xr1, ts1, tr1,
                  es2, er2, xs2, xr2, ts2, tr2, ps, pr, ys, yr, fs, fr):
     n_steps, n_batch, width = hid_hbm.shape
     n_half = n_batch // N_HALF
@@ -252,7 +254,14 @@
     def remote(src, dst, ssem, rsem, dev):
         return pltpu.make_async_remote_copy(src_ref=src, dst_ref=dst, send_sem=ssem, recv_sem=rsem, device_id=dev, device_id_type=mesh_id)
 
-    lds = [pltpu.make_async_copy(hid_hbm.at[sp], hid, ld_sem)]
+    send_to = 1 - core
+    o_cps, ml_cps = [], []
+    for q, step in enumerate(((1 - row) * 2 + send_to, row * 2 + send_to, (1 - row) * 2 + core, row * 2 + core)):
+        o_cps.append(pltpu.make_async_copy(o_hbm.at[pl.ds(step * 4, 4)], o_own.at[pl.ds(step * 4, 4)], ld_sem.at[q]))
+    ml_cp = pltpu.make_async_copy(ml_hbm, ml_own, ld_sem.at[4])
+    hid_cp = pltpu.make_async_copy(hid_hbm.at[sp], hid, ld_sem.at[5])
+    mn_cp = pltpu.make_async_copy(mn_hbm, mn_ref, ld_sem.at[6])
+    lds = [ml_cp] + o_cps + [hid_cp, mn_cp]
     wts = [pltpu.make_async_copy(a, b, w_sem.at[j]) for j, (a, b) in enumerate(((wo_hbm, wo), (wg_hbm, wg), (wu_hbm, wu), (wd_hbm, wd)))]
     for cp in lds:
         cp.start()
@@ -272,11 +281,11 @@
         pl.semaphore_signal(barrier, inc=1, device_id=to_mid, device_id_type=mesh_id)
         pl.semaphore_wait(barrier, 3)
 
-    for cp in lds:
-        cp.wait()
+    ml_cp.wait()
     a1 = []
     for q, jy in enumerate((1 - row, row)):
         step = jy * 2 + 1 - core
+        o_cps[q].wait()
         a1.append((remote(ml_own.at[step], mla.at[q], a1_snd.at[2 * q], a1_rcv.at[2 * q], partner),
                    remote(o_own.at[pl.ds(step * 4, 4)], oa.at[q], a1_snd.at[2 * q + 1], a1_rcv.at[2 * q + 1], partner)))
         for cp in a1[-1]:
@@ -300,6 +309,8 @@
             for k in range(4):
                 dst[h, k] = o_own[step * 4 + k, rs, :] * wa[:, k:k + 1] + oa[q, k, rs, :] * wb[:, k:k + 1]
 
+    for cp in lds[3:]:
+        cp.wait()
     merge_core(0, (1 - row) * 2 + core, om, mlm)
     a2 = []
     for h in range(N_HALF):
@@ -322,7 +333,7 @@
     y_cp = lambda t: remote(ob.at[t], yb.at[t], ys.at[t], yr.at[t], across)
     f_cp = lambda t: remote(yb.at[t], pf.at[t], fs.at[t], fr.at[t], partner)
 
-    def spread(h, lhs, w, dst, cp):
+    def spread(h, lhs, w, dst, cp, after=None):
         wide = width // 2
         per = N_COL // 2
         for j in range(2):
@@ -335,6 +346,9 @@
                 @pl.loop(h * N_COL + j * per, h * N_COL + (j + 1) * per)
                 def _(t):
                     cp(t).start()
+
+            if after is not None:
+                after(h)
 
     for h in range(N_HALF):
         for cp in a2[h]:
@@ -377,14 +391,59 @@
             def _(t):
                 t1_cp(t).wait_recv()
 
+    def share(t):
+        p_cp(t).start()
+        y_cp(t).start()
+
+    def relay(t):
+        y_cp(t).wait_recv()
+        f_cp(t).start()
+
+    def share_step(s):
+        @pl.when(s < n_piece)
+        def _():
+            e2_cp(s).wait_recv()
+            p2[s] = p2[s] + e2[s]
+            x2_cp(s).start()
+
+        @pl.when((s >= LAG) & (s < n_piece + LAG))
+        def _():
+            t = s - LAG
+            x2_cp(t).wait_recv()
+            o = r1[t] + (p2[t] + x2[t])
+            ob[t] = o.astype(jnp.bfloat16).astype(jnp.float32)
+            t2_cp(t).start()
+            share(t)
+
+        @pl.when(s >= LAG + LAG_Y)
+        def _():
+            relay(s - LAG - LAG_Y)
+
+
+    def share_steps(lo, hi):
+        @pl.when(is_mid)
+        def _():
+            pl.loop(lo, hi)(share_step)
+
     gain = gain_row(mn_ref)
     ffn = wg.shape[1]
-    blk = ffn // 3
-    done = 0
+    blk = ffn // TILES
+    done = [0, 0]
+
+    def serve(h):
+        for _ in range(SERVE):
+            if done[0] < n_piece + LAG:
+                sum_steps(done[0], done[0] + 1)
+                done[0] += 1
+            elif done[1] < h * N_COL:
+                share_steps(done[1], done[1] + 1)
+                done[1] += 1
+
     for h in range(N_HALF):
-        stop = (h + 1) * N_COL + LAG
-        sum_steps(done, stop)
-        done = stop
+        stop = max(done[0], (h + 1) * N_COL + LAG)
+        if stop > done[0]:
+            sum_steps(done[0], stop)
+            done[0] = stop
         end_recv(h * N_COL, (h + 1) * N_COL)
         sq = jnp.zeros((n_half, 1), jnp.float32)
         for n in range(N_COL):
@@ -396,48 +455,17 @@
         if h == 0:
             wts[1].wait()
             wts[2].wait()
-        for n in range(3):
+        for n in range(TILES):
             cs = slice(n * blk, (n + 1) * blk)
             g = jnp.dot(m_s[...], wg[:, cs], preferred_element_type=jnp.float32)
             u = jnp.dot(m_s[...], wu[:, cs], preferred_element_type=jnp.float32)
             act[:, cs] = (jax.nn.silu(g) * u).astype(jnp.bfloat16)
-            if h + 1 < N_HALF:
-                sum_steps(done, done + 2)
-                done += 2
+            serve(h)
         if h == 0:
             wts[3].wait()
-        spread(h, act[...], wd, p2, e2_cp)
-
-    def share(t):
-        p_cp(t).start()
-        y_cp(t).start()
-
-    def relay(t):
-        y_cp(t).wait_recv()
-        f_cp(t).start()
-
-    @pl.when(is_mid)
-    def _():
-        @pl.loop(0, n_piece + LAG + LAG_Y)
-        def _(s):
-            @pl.when(s < n_piece)
-            def _():
-                e2_cp(s).wait_recv()
-                p2[s] = p2[s] + e2[s]
-                x2_cp(s).start()
-
-            @pl.when((s >= LAG) & (s < n_piece + LAG))
-            def _():
-                t = s - LAG
-                x2_cp(t).wait_recv()
-                o = r1[t] + (p2[t] + x2[t])
-                ob[t] = o.astype(jnp.bfloat16).astype(jnp.float32)
-                t2_cp(t).start()
-                share(t)
-
-            @pl.when(s >= LAG + LAG_Y)
-            def _():
-                relay(s - LAG - LAG_Y)
+        spread(h, act[...], wd, p2, e2_cp, serve)
+
+    share_steps(done[1], n_piece + LAG + LAG_Y)
 
     @pl.when(is_end)
     def _():
@@ -452,17 +480,32 @@
             def _():
                 relay(s - LAG_Y)
 
-    @pl.loop(0, n_piece)
-    def _(t):
+    def put(j, t, val):
         h = t // N_COL
         rs = pl.ds(pl.multiple_of(h * n_half, n_half), n_half)
         cs = pl.ds(pl.multiple_of((t - h * N_COL) * n_col, n_col), n_col)
-        out_ref[sp, rs, cs] = ob[t].astype(jnp.bfloat16)
-        out_ref[(1 - row) * 2 + core, rs, cs] = yb[t].astype(jnp.bfloat16)
-        p_cp(t).wait_recv()
-        out_ref[row * 2 + 1 - core, rs, cs] = pb[t].astype(jnp.bfloat16)
-        f_cp(t).wait_recv()
-        out_ref[(1 - row) * 2 + 1 - core, rs, cs] = pf[t].astype(jnp.bfloat16)
+        out_ref[j, rs, cs] = val.astype(jnp.bfloat16)
+
+    def leave(j, h, k):
+        rs = pl.ds(h * n_half, n_half)
+        return pltpu.make_async_copy(out_ref.at[j, rs], out_hbm.at[j, rs], out_sem.at[h * 4 + k])
+
+    homes = (sp, row * 2 + 1 - core, (1 - row) * 2 + core, (1 - row) * 2 + 1 - core)
+    for h in range(N_HALF):
+        @pl.loop(h * N_COL, (h + 1) * N_COL)
+        def _(t):
+            put(homes[0], t, ob[t])
+            p_cp(t).wait_recv()
+            put(homes[1], t, pb[t])
+            put(homes[2], t, yb[t])
+            f_cp(t).wait_recv()
+            put(homes[3], t, pf[t])
+
+        for k in range(4):
+            leave(homes[k], h, k).start()
+
+    @pl.loop(0, n_piece)
+    def _(t):
         p_cp(t).wait_send()
         y_cp(t).wait_send()
         f_cp(t).wait_send()
@@ -478,6 +521,10 @@
         def _():
             e1_cp(t).wait_send()
             e2_cp(t).wait_send()
+
+    for h in range(N_HALF):
+        for k in range(4):
+            leave(homes[k], h, k).wait()
 
 
 def layer(o, ml, hidden, w_o, w_gate, w_up, w_down, mlp_norm):
@@ -494,9 +541,13 @@
         layer_kernel,
         name='layer',
         out_shape=jax.ShapeDtypeStruct(hidden.shape, bf16),
-        in_specs=[vm] * 2 + [anyspec] * 5 + [vm],
-        out_specs=vm,
+        in_specs=[anyspec] * 8,
+        out_specs=anyspec,
         scratch_shapes=[
+            pltpu.VMEM((16, n_batch, HEAD), f32),
+            pltpu.VMEM((4, n_batch, HEAD), f32),
+            pltpu.VMEM((width // HEAD, HEAD), bf16),
+            pltpu.VMEM(hidden.shape, bf16),
             pltpu.VMEM((2, 4, n_batch, HEAD), f32),
             pltpu.VMEM((2, n_batch, HEAD), f32),
             pltpu.VMEM((N_HALF, 4, n_half, HEAD), f32),
@@ -515,7 +566,7 @@
             pltpu.VMEM((n_half, width), bf16),
             pltpu.VMEM((n_half, w_gate.shape[1]), bf16),
             piece, piece, piece, piece, piece, piece, piece,
-            dma, dma((4,)), dma((4,)), dma((4,)), dma((2 * N_HALF,)), dma((2 * N_HALF,)),
+            dma((7,)), dma((4 * N_HALF,)), dma((4,)), dma((4,)), dma((4,)), dma((2 * N_HALF,)), dma((2 * N_HALF,)),
         ] + [dma((n_piece,))] * 18,
         compiler_params=pltpu.CompilerParams(collective_id=0, has_side_effects=True, vmem_limit_bytes=67043328),
         cost_estimate=pl.CostEstimate(flops=2 * 10 ** 9, bytes_accessed=30 * 10 ** 6, transcendentals=10 ** 6),

time: 73.4 us -> 69.4 us (0.946)
  Pallas kernels: 70.1 us -> 66.2 us
    pallas_call x1, Pallas kernels: 54.8 us -> 50.9 us  [layer(): pl.pallas_call(layer_kernel, name='layer', out_shape=jax.ShapeDtypeStruct...]
where the time goes in v4:
time: 69.4 us; the launch traced here: 69.2 us
  Pallas kernels  66.2 us (95%)
  local copies, waits for them, and re-layouts  2.3 us (3%)
    pallas_call x1, Pallas kernels, layer(): pl.pallas_call(layer_kernel, name='layer', out_shape=jax.ShapeDtypeStruct...  50.9 us
    pallas_call x1, Pallas kernels, attend(): pl.pallas_call(attend_kernel, name='attend', out_shape=(jax.ShapeDtypeStr...  15.3 us
    unnamed x1, local copies, waits for them, and re-layouts  2.3 us

profile of v4, /device:TPU:1, one launch (start us, length us, event | category | flops | bytes accessed | tf_op | source)
XLA Modules:
  0.0 69.2 jit_solution(5209553175425266227)
XLA Ops:
  0.6 15.3 %attend.1 = (f32[1024,128]{1,0:T(8,128)}, f32[4,64,128]{2,1,0:T(8,128)}, bf16[64,512,128]{2,1,0:T(8,128)(2,1)}, bf16[64,512,128]{2,1,0:T(8,128)(2,1)}) custom-call(s32[64]{0:T(128)} %start_ref.1, bf16[4,64,2048]{2,1,0:T(8,128)(2,1)} %hid_hbm.3, bf16[2048,512]{1,0:T(8,128)(2,1)} %wq_hbm.1, bf16[2048,256]{1,0:T(8,128)(2,1)} %wk_hbm.1, ...), custom_call_target="tpu_custom_call" | custom-call | flops 2000000000 | bytes 40000000 | tf_op jit(solution)/shard_map/attend/pallas_call | solution.py:186
  15.9 50.9 %layer.1 = bf16[4,64,2048]{2,1,0:T(8,128)(2,1)} custom-call(f32[16,64,128]{2,1,0:T(8,128)} %bitcast.11, f32[4,64,128]{2,1,0:T(8,128)} %get-tuple-element.8.ml_hbm, bf16[4,64,2048]{2,1,0:T(8,128)(2,1)} %hid_hbm.3, bf16[512,2048]{1,0:T(8,128)(2,1)} %wo_hbm.1, bf16[2048,1536]{1,0:T(8,128)(2,1)} %wg_hbm.1, bf16[2048,1536]{1,0:T(8,128)(2,1)} %wu_hbm.1, ...), custom_call_target="tpu_custom_call" | custom-call | flops 2000000000 | bytes 30000000 | tf_op jit(solution)/shard_map/layer/pallas_call | solution.py:540
  66.9 2.3 %copy.20 = bf16[4,64,2048]{2,1,0:T(8,128)(2,1)} copy(bf16[4,64,2048]{2,1,0:T(8,128)(2,1)} %layer.1) | data formatting | bytes 2097152

commit v5 on v4

--- a/solution.py
+++ b/solution.py
@@ -19,8 +19,9 @@
     return jnp.concatenate([g[j:j + 1] for j in range(g.shape[0])], axis=1)
 
 
-def attend_kernel(start_ref, hid_hbm, wq_hbm, wk_hbm, wv_hbm, kc_hbm, vc_hbm, an_ref, qg_ref, kg_ref, freq_ref,
-                  o_ref, ml_ref, ko_hbm, vo_hbm,
+def attend_kernel(start_hbm, hid_hbm, wq_hbm, wk_hbm, wv_hbm, kc_hbm, vc_hbm, an_hbm, qg_hbm, kg_hbm, freq_hbm,
+                  o_hbm, ml_hbm, ko_hbm, vo_hbm,
+                  start_ref, an_ref, qg_ref, kg_ref, freq_ref, o_ref, ml_ref, s_sem, o_sem,
                   hid, wq, wk, wv, kbuf, vbuf, nrm, raw, q_s, k_s, v_s, pos_s, ml_s, key_s, sc_s, pr_s,
                   w_sem, h_sem, kin_sem, vin_sem, kout_sem, vout_sem):
     n_steps, n_batch, width = hid.shape
@@ -32,8 +33,11 @@
     blk_start = lax.axis_index('sp') * seq_blk
     scale = HEAD ** -0.5
 
+    small = [pltpu.make_async_copy(a, b, s_sem.at[j]) for j, (a, b) in enumerate((
+        (start_hbm, start_ref), (freq_hbm, freq_ref), (an_hbm, an_ref), (qg_hbm, qg_ref), (kg_hbm, kg_ref)))]
     hid_cp = pltpu.make_async_copy(hid_hbm, hid, h_sem)
-    hid_cp.start()
+    for cp in small[:2] + [hid_cp] + small[2:]:
+        cp.start()
     w_cps = [pltpu.make_async_copy(a, b, w_sem.at[j]) for j, (a, b) in enumerate(((wq_hbm, wq), (wk_hbm, wk), (wv_hbm, wv)))]
     for cp in w_cps:
         cp.start()
@@ -53,6 +57,9 @@
         a, b = kv_in(c)
         a.start()
         b.start()
+
+    for cp in small:
+        cp.wait()
 
     @pl.loop(0, n_batch)
     def _(b):
@@ -165,12 +172,18 @@
     for i in range(n_steps):
         ml = ml_s[...]
         ml_ref[i] = ml if i == 0 else pltpu.roll(ml, HEAD - 4 * i, 1)
+    outs = [pltpu.make_async_copy(o_ref, o_hbm, o_sem.at[0]), pltpu.make_async_copy(ml_ref, ml_hbm, o_sem.at[1])]
+    for cp in outs:
+        cp.start()
 
     @pl.loop(0, n_chunk)
     def _(c):
         a, b = kv_out(c)
         a.wait()
         b.wait()
+
+    for cp in outs:
+        cp.wait()
 
 
 def attend(start_pos, hidden, w_q, w_k, w_v, k_cache, v_cache, attn_norm, q_gain, k_gain):
@@ -181,7 +194,6 @@
     half = HEAD // 2
     f = ROPE_BASE ** (-(np.arange(half, dtype=np.float64) * (2.0 / HEAD)))
     freq = np.stack([np.concatenate([f, f]), np.concatenate([-np.ones(half), np.ones(half)])]).astype(np.float32)
-    vm = pl.BlockSpec(memory_space=pltpu.VMEM)
     anyspec = pl.BlockSpec(memory_space=pltpu.HBM)
     return pl.pallas_call(
         attend_kernel,
@@ -190,9 +202,18 @@
                    jax.ShapeDtypeStruct((n_steps, n_batch, HEAD), jnp.float32),
                    jax.ShapeDtypeStruct(k_cache.shape, jnp.bfloat16),
                    jax.ShapeDtypeStruct(v_cache.shape, jnp.bfloat16)),
-        in_specs=[pl.BlockSpec(memory_space=pltpu.SMEM)] + [anyspec] * 6 + [vm] * 4,
-        out_specs=(vm, vm, anyspec, anyspec),
+        in_specs=[anyspec] * 11,
+        out_specs=(anyspec,) * 4,
         scratch_shapes=[
+            pltpu.SMEM(start_pos.shape, jnp.int32),
+            pltpu.VMEM((width // HEAD, HEAD), jnp.bfloat16),
+            pltpu.VMEM((1, HEAD), jnp.bfloat16),
+            pltpu.VMEM((1, HEAD), jnp.bfloat16),
+            pltpu.VMEM((2, HEAD), jnp.float32),
+            pltpu.VMEM((16 * n_batch, HEAD), jnp.float32),
+            pltpu.VMEM((n_steps, n_batch, HEAD), jnp.float32),
+            pltpu.SemaphoreType.DMA((5,)),
+            pltpu.SemaphoreType.DMA((2,)),
             pltpu.VMEM(hidden.shape, jnp.bfloat16),
             pltpu.VMEM(w_q.shape, jnp.bfloat16),
             pltpu.VMEM(w_k.shape, jnp.bfloat16),

time: 69.4 us -> 67.6 us (0.974)
  Pallas kernels: 66.2 us -> 64.5 us
    pallas_call x1, Pallas kernels: 15.3 us -> 13.6 us  [attend(): pl.pallas_call(attend_kernel, name='attend', out_shape=(jax.ShapeDtypeStr...]
where the time goes in v5:
time: 67.6 us; the launch traced here: 67.5 us
  Pallas kernels  64.5 us (95%)
  local copies, waits for them, and re-layouts  2.3 us (3%)
    pallas_call x1, Pallas kernels, layer(): pl.pallas_call(layer_kernel, name='layer', out_shape=jax.ShapeDtypeStruct...  50.9 us
    pallas_call x1, Pallas kernels, attend(): pl.pallas_call(attend_kernel, name='attend', out_shape=(jax.ShapeDtypeStr...  13.6 us
    unnamed x1, local copies, waits for them, and re-layouts  2.3 us

profile of v5, /device:TPU:1, one launch (start us, length us, event | category | flops | bytes accessed | tf_op | source)
XLA Modules:
  0.0 67.5 jit_solution(8661411191760992474)
XLA Ops:
  0.6 13.6 %attend.1 = (f32[1024,128]{1,0:T(8,128)}, f32[4,64,128]{2,1,0:T(8,128)}, bf16[64,512,128]{2,1,0:T(8,128)(2,1)}, bf16[64,512,128]{2,1,0:T(8,128)(2,1)}) custom-call(s32[64]{0:T(128)} %start_hbm.1, bf16[4,64,2048]{2,1,0:T(8,128)(2,1)} %hid_hbm.3, bf16[2048,512]{1,0:T(8,128)(2,1)} %wq_hbm.1, bf16[2048,256]{1,0:T(8,128)(2,1)} %wk_hbm.1, ...), custom_call_target="tpu_custom_call" | custom-call | flops 2000000000 | bytes 40000000 | tf_op jit(solution)/shard_map/attend/pallas_call | solution.py:198
  14.2 50.9 %layer.1 = bf16[4,64,2048]{2,1,0:T(8,128)(2,1)} custom-call(f32[16,64,128]{2,1,0:T(8,128)} %bitcast.11, f32[4,64,128]{2,1,0:T(8,128)} %get-tuple-element.8.ml_hbm, bf16[4,64,2048]{2,1,0:T(8,128)(2,1)} %hid_hbm.3, bf16[512,2048]{1,0:T(8,128)(2,1)} %wo_hbm.1, bf16[2048,1536]{1,0:T(8,128)(2,1)} %wg_hbm.1, bf16[2048,1536]{1,0:T(8,128)(2,1)} %wu_hbm.1, ...), custom_call_target="tpu_custom_call" | custom-call | flops 2000000000 | bytes 30000000 | tf_op jit(solution)/shard_map/layer/pallas_call | solution.py:561
  65.2 2.3 %copy.20 = bf16[4,64,2048]{2,1,0:T(8,128)(2,1)} copy(bf16[4,64,2048]{2,1,0:T(8,128)(2,1)} %layer.1) | data formatting | bytes 2097152

commit v6 on v5

--- a/solution.py
+++ b/solution.py
@@ -246,8 +246,8 @@
 N_HALF = 4
 LAG = 5
 LAG_Y = 8
-TILES = 3
-SERVE = 1
+TILES = 2
+SERVE = 2
 
 
 def layer_kernel(o_hbm, ml_hbm, hid_hbm, wo_hbm, wg_hbm, wu_hbm, wd_hbm, mn_hbm, out_hbm,
@@ -275,6 +275,19 @@
     def remote(src, dst, ssem, rsem, dev):
         return pltpu.make_async_remote_copy(src_ref=src, dst_ref=dst, send_sem=ssem, recv_sem=rsem, device_id=dev, device_id_type=mesh_id)
 
+    barrier = pltpu.get_barrier_semaphore()
+    for dev in (partner, across):
+        pl.semaphore_signal(barrier, inc=1, device_id=dev, device_id_type=mesh_id)
+
+    @pl.when(is_mid)
+    def _():
+        pl.semaphore_signal(barrier, inc=1, device_id=to_end, device_id_type=mesh_id)
+        pl.semaphore_signal(barrier, inc=1, device_id=to_other, device_id_type=mesh_id)
+
+    @pl.when(is_end)
+    def _():
+        pl.semaphore_signal(barrier, inc=1, device_id=to_mid, device_id_type=mesh_id)
+
     send_to = 1 - core
     o_cps, ml_cps = [], []
     for q, step in enumerate(((1 - row) * 2 + send_to, row * 2 + send_to, (1 - row) * 2 + core, row * 2 + core)):
@@ -287,19 +300,12 @@
     for cp in lds:
         cp.start()
 
-    barrier = pltpu.get_barrier_semaphore()
-    for dev in (partner, across):
-        pl.semaphore_signal(barrier, inc=1, device_id=dev, device_id_type=mesh_id)
-
     @pl.when(is_mid)
     def _():
-        pl.semaphore_signal(barrier, inc=1, device_id=to_end, device_id_type=mesh_id)
-        pl.semaphore_signal(barrier, inc=1, device_id=to_other, device_id_type=mesh_id)
         pl.semaphore_wait(barrier, 4)
 
     @pl.when(is_end)
     def _():
-        pl.semaphore_signal(barrier, inc=1, device_id=to_mid, device_id_type=mesh_id)
         pl.semaphore_wait(barrier, 3)
 
     ml_cp.wait()
@@ -320,7 +326,7 @@
         tot = pltpu.roll(ma, HEAD - 16, 1) * wa + pltpu.roll(mb, HEAD - 16, 1) * wb
         return top, wa, wb, tot
 
-    def merge_core(q, step, dst, mldst):
+    def merge_core(q, step, dst, mldst, send=None):
         for cp in a1[q]:
             cp.wait()
         for h in range(N_HALF):
@@ -329,16 +335,17 @@
             mldst[h] = jnp.where(lane < 16, top, pltpu.roll(tot, 16, 1))
             for k in range(4):
                 dst[h, k] = o_own[step * 4 + k, rs, :] * wa[:, k:k + 1] + oa[q, k, rs, :] * wb[:, k:k + 1]
+            if send is not None:
+                for cp in send[h]:
+                    cp.start()
 
     for cp in lds[3:]:
         cp.wait()
-    merge_core(0, (1 - row) * 2 + core, om, mlm)
     a2 = []
     for h in range(N_HALF):
         a2.append((remote(mlm.at[h], mly.at[h], a2_snd.at[2 * h], a2_rcv.at[2 * h], across),
                    remote(om.at[h], oy.at[h], a2_snd.at[2 * h + 1], a2_rcv.at[2 * h + 1], across)))
-        for cp in a2[-1]:
-            cp.start()
+    merge_core(0, (1 - row) * 2 + core, om, mlm, a2)
     for cp in wts:
         cp.start()
     merge_core(1, row * 2 + core, own, ml_mine)
@@ -594,6 +601,34 @@
     )(o.reshape(16, n_batch, HEAD), ml, hidden, w_o, w_gate, w_up, w_down, mlp_norm.reshape(-1, HEAD))
 
 
+def emit_kernel(src, dst, buf, in_sem, out_sem):
+    n = buf.shape[0]
+    ins = [pltpu.make_async_copy(src.at[j], buf.at[j], in_sem.at[j]) for j in range(n)]
+    outs = [pltpu.make_async_copy(buf.at[j], dst.at[j], out_sem.at[j]) for j in range(n)]
+    for cp in ins:
+        cp.start()
+    for j in range(n):
+        ins[j].wait()
+        outs[j].start()
+    for cp in outs:
+        cp.wait()
+
+
+def emit(x):
+    n = x.shape[0]
+    anyspec = pl.BlockSpec(memory_space=pltpu.HBM)
+    return pl.pallas_call(
+        emit_kernel,
+        name='emit',
+        out_shape=jax.ShapeDtypeStruct(x.shape, x.dtype),
+        in_specs=[anyspec],
+        out_specs=anyspec,
+        scratch_shapes=[pltpu.VMEM(x.shape, x.dtype), pltpu.SemaphoreType.DMA((n,)), pltpu.SemaphoreType.DMA((n,))],
+        compiler_params=pltpu.CompilerParams(vmem_limit_bytes=67043328),
+        cost_estimate=pl.CostEstimate(flops=0, bytes_accessed=4 * 10 ** 6, transcendentals=0),
+    )(x)
+
+
 def solution(mesh):
     cache_spec = P('dp', 'sp', 'tp', None)
     col_spec = P(None, 'tp')
@@ -606,6 +641,6 @@
         flat = (k_cache.shape[0], k_cache.shape[1] * k_cache.shape[2], k_cache.shape[3])
         o, ml, k_out, v_out = attend(start_pos, hidden, w_q, w_k, w_v, k_cache.reshape(flat), v_cache.reshape(flat), attn_norm, q_gain, k_gain)
         out = layer(o, ml, hidden, w_o, w_gate, w_up, w_down, mlp_norm)
-        return out, k_out.reshape(k_cache.shape), v_out.reshape(v_cache.shape)
+        return emit(out), k_out.reshape(k_cache.shape), v_out.reshape(v_cache.shape)
 
     return jax.shard_map(shard_body, mesh=mesh, in_specs=in_specs, out_specs=out_specs, check_vma=False)

time: 67.6 us -> 67.1 us (level)
  local copies, waits for them, and re-layouts: 2.3 us -> 0 us
  Pallas kernels: 64.5 us -> 66.3 us
    unnamed x1 -> x0, local copies, waits for them, and re-layouts: 2.3 us -> none
    pallas_call x0 -> x1, Pallas kernels: none -> 1.98 us  [emit(): pl.pallas_call(emit_kernel, name='emit', out_shape=jax.ShapeDtypeStruct(x...]
where the time goes in v6:
time: 67.1 us; the launch traced here: 66.9 us
  Pallas kernels  66.3 us (99%)
    pallas_call x1, Pallas kernels, layer(): pl.pallas_call(layer_kernel, name='layer', out_shape=jax.ShapeDtypeStruct...  50.7 us
    pallas_call x1, Pallas kernels, attend(): pl.pallas_call(attend_kernel, name='attend', out_shape=(jax.ShapeDtypeStr...  13.6 us
    pallas_call x1, Pallas kernels, emit(): pl.pallas_call(emit_kernel, name='emit', out_shape=jax.ShapeDtypeStruct(x...  1.98 us

profile of v6, /device:TPU:1, one launch (start us, length us, event | category | flops | bytes accessed | tf_op | source)
XLA Modules:
  0.0 66.9 jit_solution(11749102095949129582)
XLA Ops:
  0.6 13.6 %attend.1 = (f32[1024,128]{1,0:T(8,128)}, f32[4,64,128]{2,1,0:T(8,128)}, bf16[64,512,128]{2,1,0:T(8,128)(2,1)}, bf16[64,512,128]{2,1,0:T(8,128)(2,1)}) custom-call(s32[64]{0:T(128)} %start_hbm.1, bf16[4,64,2048]{2,1,0:T(8,128)(2,1)} %hid_hbm.3, bf16[2048,512]{1,0:T(8,128)(2,1)} %wq_hbm.1, bf16[2048,256]{1,0:T(8,128)(2,1)} %wk_hbm.1, ...), custom_call_target="tpu_custom_call" | custom-call | flops 2000000000 | bytes 40000000 | tf_op jit(solution)/shard_map/attend/pallas_call | solution.py:198
  14.2 50.7 %layer.1.src = bf16[4,64,2048]{2,1,0:T(8,128)(2,1)} custom-call(f32[16,64,128]{2,1,0:T(8,128)} %bitcast.11, f32[4,64,128]{2,1,0:T(8,128)} %get-tuple-element.8.ml_hbm, bf16[4,64,2048]{2,1,0:T(8,128)(2,1)} %hid_hbm.3, bf16[512,2048]{1,0:T(8,128)(2,1)} %wo_hbm.1, bf16[2048,1536]{1,0:T(8,128)(2,1)} %wg_hbm.1, bf16[2048,1536]{1,0:T(8,128)(2,1)} %wu_hbm.1, ...), custom_call_target="tpu_custom_call" | custom-call | flops 2000000000 | bytes 30000000 | tf_op jit(solution)/shard_map/layer/pallas_call | solution.py:568
  64.9 2.0 %emit.1 = bf16[4,64,2048]{2,1,0:T(8,128)(2,1)} custom-call(bf16[4,64,2048]{2,1,0:T(8,128)(2,1)} %layer.1.src), custom_call_target="tpu_custom_call" | custom-call | bytes 4000000 | tf_op jit(solution)/shard_map/emit/pallas_call | solution.py:620

commit v7 on v6

--- a/solution.py
+++ b/solution.py
@@ -9,7 +9,7 @@
 
 ROPE_BASE = 1000000.0
 NORM_EPS = 1e-06
-NEG_BIG = -1e30
+NEG_BIG = -3e38
 HEAD = 128
 CHUNK = 8
 
@@ -420,8 +420,8 @@
                 t1_cp(t).wait_recv()
 
     def share(t):
+        y_cp(t).start()
         p_cp(t).start()
-        y_cp(t).start()
 
     def relay(t):
         y_cp(t).wait_recv()

time: 67.1 us -> 67.1 us (level)
  no operation moved by 1% of the time
where the time goes in v7:
time: 67.1 us; the launch traced here: 66.9 us
  Pallas kernels  66.3 us (99%)
    pallas_call x1, Pallas kernels, layer(): pl.pallas_call(layer_kernel, name='layer', out_shape=jax.ShapeDtypeStruct...  50.7 us
    pallas_call x1, Pallas kernels, attend(): pl.pallas_call(attend_kernel, name='attend', out_shape=(jax.ShapeDtypeStr...  13.6 us
    pallas_call x1, Pallas kernels, emit(): pl.pallas_call(emit_kernel, name='emit', out_shape=jax.ShapeDtypeStruct(x...  1.98 us

profile of v7, /device:TPU:1, one launch (start us, length us, event | category | flops | bytes accessed | tf_op | source)
XLA Modules:
  0.0 66.9 jit_solution(15948148367679912299)
XLA Ops:
  0.6 13.6 %attend.1 = (f32[1024,128]{1,0:T(8,128)}, f32[4,64,128]{2,1,0:T(8,128)}, bf16[64,512,128]{2,1,0:T(8,128)(2,1)}, bf16[64,512,128]{2,1,0:T(8,128)(2,1)}) custom-call(s32[64]{0:T(128)} %start_hbm.1, bf16[4,64,2048]{2,1,0:T(8,128)(2,1)} %hid_hbm.3, bf16[2048,512]{1,0:T(8,128)(2,1)} %wq_hbm.1, bf16[2048,256]{1,0:T(8,128)(2,1)} %wk_hbm.1, ...), custom_call_target="tpu_custom_call" | custom-call | flops 2000000000 | bytes 40000000 | tf_op jit(solution)/shard_map/attend/pallas_call | solution.py:198
  14.2 50.7 %layer.1.src = bf16[4,64,2048]{2,1,0:T(8,128)(2,1)} custom-call(f32[16,64,128]{2,1,0:T(8,128)} %bitcast.11, f32[4,64,128]{2,1,0:T(8,128)} %get-tuple-element.8.ml_hbm, bf16[4,64,2048]{2,1,0:T(8,128)(2,1)} %hid_hbm.3, bf16[512,2048]{1,0:T(8,128)(2,1)} %wo_hbm.1, bf16[2048,1536]{1,0:T(8,128)(2,1)} %wg_hbm.1, bf16[2048,1536]{1,0:T(8,128)(2,1)} %wu_hbm.1, ...), custom_call_target="tpu_custom_call" | custom-call | flops 2000000000 | bytes 30000000 | tf_op jit(solution)/shard_map/layer/pallas_call | solution.py:568
  64.9 2.0 %emit.1 = bf16[4,64,2048]{2,1,0:T(8,128)(2,1)} custom-call(bf16[4,64,2048]{2,1,0:T(8,128)(2,1)} %layer.1.src), custom_call_target="tpu_custom_call" | custom-call | bytes 4000000 | tf_op jit(solution)/shard_map/emit/pallas_call | solution.py:620

commit v8 on v7

--- a/solution.py
+++ b/solution.py
@@ -389,16 +389,19 @@
 
         spread(h, attn[h], wo, p1, e1_cp)
 
-    def sum_step(s):
+    def sum_step(s, lag):
         @pl.when(s < n_piece)
         def _():
             e1_cp(s).wait_recv()
             p1[s] = p1[s] + e1[s]
             x1_cp(s).start()
 
-        @pl.when(s >= LAG)
-        def _():
-            t = s - LAG
+        if lag is None:
+            return
+
+        @pl.when(s >= lag)
+        def _():
+            t = s - lag
             h = t // N_COL
             rs = pl.ds(pl.multiple_of(h * n_half, n_half), n_half)
             cs = pl.ds(pl.multiple_of((t - h * N_COL) * n_col, n_col), n_col)
@@ -407,10 +410,10 @@
             r1[t] = r.astype(jnp.bfloat16).astype(jnp.float32)
             t1_cp(t).start()
 
-    def sum_steps(lo, hi):
+    def sum_steps(lo, hi, lag=LAG):
         @pl.when(is_mid)
         def _():
-            pl.loop(lo, hi)(sum_step)
+            pl.loop(lo, hi)(lambda s: sum_step(s, lag))
 
     def end_recv(lo, hi):
         @pl.when(is_end)
@@ -457,20 +460,21 @@
     ffn = wg.shape[1]
     blk = ffn // TILES
     done = [0, 0]
+    early = N_COL + LAG - 1
 
     def serve(h):
         for _ in range(SERVE):
             if done[0] < n_piece + LAG:
-                sum_steps(done[0], done[0] + 1)
+                sum_steps(done[0], done[0] + 1, None if done[0] == early else LAG)
                 done[0] += 1
             elif done[1] < h * N_COL:
                 share_steps(done[1], done[1] + 1)
                 done[1] += 1
 
     for h in range(N_HALF):
-        stop = max(done[0], (h + 1) * N_COL + LAG)
+        stop = early if h == 0 else max(done[0], (h + 1) * N_COL + LAG)
         if stop > done[0]:
-            sum_steps(done[0], stop)
+            sum_steps(done[0], stop, LAG - 1 if h == 0 else LAG)
             done[0] = stop
         end_recv(h * N_COL, (h + 1) * N_COL)
         sq = jnp.zeros((n_half, 1), jnp.float32)

time: 67.1 us -> 66.5 us (level)
  no operation moved by 1% of the time
where the time goes in v8:
time: 66.5 us; the launch traced here: 66.4 us
  Pallas kernels  65.7 us (99%)
    pallas_call x1, Pallas kernels, layer(): pl.pallas_call(layer_kernel, name='layer', out_shape=jax.ShapeDtypeStruct...  50.2 us
    pallas_call x1, Pallas kernels, attend(): pl.pallas_call(attend_kernel, name='attend', out_shape=(jax.ShapeDtypeStr...  13.6 us
    pallas_call x1, Pallas kernels, emit(): pl.pallas_call(emit_kernel, name='emit', out_shape=jax.ShapeDtypeStruct(x...  1.98 us

profile of v8, /device:TPU:1, one launch (start us, length us, event | category | flops | bytes accessed | tf_op | source)
XLA Modules:
  0.0 66.4 jit_solution(4533779454636666798)
XLA Ops:
  0.6 13.6 %attend.1 = (f32[1024,128]{1,0:T(8,128)}, f32[4,64,128]{2,1,0:T(8,128)}, bf16[64,512,128]{2,1,0:T(8,128)(2,1)}, bf16[64,512,128]{2,1,0:T(8,128)(2,1)}) custom-call(s32[64]{0:T(128)} %start_hbm.1, bf16[4,64,2048]{2,1,0:T(8,128)(2,1)} %hid_hbm.3, bf16[2048,512]{1,0:T(8,128)(2,1)} %wq_hbm.1, bf16[2048,256]{1,0:T(8,128)(2,1)} %wk_hbm.1, ...), custom_call_target="tpu_custom_call" | custom-call | flops 2000000000 | bytes 40000000 | tf_op jit(solution)/shard_map/attend/pallas_call | solution.py:198
  14.2 50.2 %layer.1.src = bf16[4,64,2048]{2,1,0:T(8,128)(2,1)} custom-call(f32[16,64,128]{2,1,0:T(8,128)} %bitcast.11, f32[4,64,128]{2,1,0:T(8,128)} %get-tuple-element.8.ml_hbm, bf16[4,64,2048]{2,1,0:T(8,128)(2,1)} %hid_hbm.3, bf16[512,2048]{1,0:T(8,128)(2,1)} %wo_hbm.1, bf16[2048,1536]{1,0:T(8,128)(2,1)} %wg_hbm.1, bf16[2048,1536]{1,0:T(8,128)(2,1)} %wu_hbm.1, ...), custom_call_target="tpu_custom_call" | custom-call | flops 2000000000 | bytes 30000000 | tf_op jit(solution)/shard_map/layer/pallas_call | solution.py:572
  64.4 2.0 %emit.1 = bf16[4,64,2048]{2,1,0:T(8,128)(2,1)} custom-call(bf16[4,64,2048]{2,1,0:T(8,128)(2,1)} %layer.1.src), custom_call_target="tpu_custom_call" | custom-call | bytes 4000000 | tf_op jit(solution)/shard_map/emit/pallas_call | solution.py:624
